TPU v7x, 128 devices: a whole 4x4x4 slice. The times are simulated.
128 devices in a mesh: grp: 2 (over core), row: 8 (over z, y_hi), col: 8 (over y_lo, x).
Axes of the slice: x: 4, y: 4 (y_hi: 2, y_lo: 2; y = y_hi * 2 + y_lo), z: 4, core: 2. Of those that a mesh axis runs over, the one named last changes fastest.
Arguments:
- ainv_anc: bfloat16 [12288, 12288], P(('grp', 'row'), 'col'), may hold values from -12 to 12
- l_upper: bfloat16 [12288, 2048], P(('grp', 'row'), 'col'), may hold values from -0.0546875 to 0.0546875
- mask_upper: int32 [8, 48], replicated, may hold values from 0 to 1, as said below
- dinv_upper: float32 [256, 2048], P(None, 'col'), may hold values from -6 to 6
- l_lower: bfloat16 [12288, 2048], P(('grp', 'row'), 'col'), may hold values from -0.0546875 to 0.0546875
- mask_lower: int32 [8, 48], replicated, may hold values from 0 to 1, as said below
- parent: int32 [8], replicated, may hold values from 0 to 7
- lp_lower: bfloat16 [256, 2048], P(None, 'col'), may hold values from -0.375 to 0.375
- dinv_lower: float32 [256, 2048], P(None, 'col'), may hold values from -6 to 6
Outputs:
- x_upper: bfloat16 [12288, 2048], P(('grp', 'row'), 'col')
- diag_upper: bfloat16 [256, 2048], P(None, 'col')
- y_lower: bfloat16 [12288, 2048], P(('grp', 'row'), 'col')
- y_parent: bfloat16 [256, 2048], P(None, 'col')
- diag_lower: bfloat16 [256, 2048], P(None, 'col')
Inputs may be any that keep to these rules, and one draw needn't show every extreme that they name: mask_upper[u, a] is 1 where ancestor block a lies in the structure of upper supernode u. mask_lower[l, a] is 1 where ancestor block a lies in the structure of lower supernode l. parent[l] is the upper supernode whose columns hold lower supernode l's parent block.
All inputs are finite; a program needn't handle non-finite values.
Results may differ from a plain program's by a relative error of at most 0.0095.
Values may be sent and summed in bfloat16 or wider, within the bound.
A program may use at most 128 MiB of HBM per device.

v0:
```python
import jax.numpy as jnp
from jax import lax

B = 256
ANC = 12288
SN = 8


def masked_panel(factor, pattern):
    height, breadth = factor.shape
    shaped = factor.reshape(height // B, B, breadth // B, B)
    keeping = (jnp.transpose(pattern) > 0)[:, None, :, None]
    return jnp.where(keeping, shaped, jnp.zeros((), factor.dtype)).reshape(height, breadth)


def reference(
    ainv_anc, l_upper, mask_upper, dinv_upper, l_lower, mask_lower, parent, lp_lower, dinv_lower
):
    precise = lax.Precision.HIGHEST
    ancestor = ainv_anc.astype(jnp.float32)
    upper_masked = masked_panel(l_upper, mask_upper)
    x_upper = (-jnp.dot(ancestor, upper_masked.astype(jnp.float32), precision=precise)).astype(
        jnp.bfloat16
    )
    upper_cube = upper_masked.astype(jnp.float32).reshape(ANC, SN, B)
    x_cube = x_upper.astype(jnp.float32).reshape(ANC, SN, B)
    upper_terms = jnp.einsum("aub,auc->buc", upper_cube, x_cube, precision=precise).reshape(
        B, SN * B
    )
    diag_upper = (dinv_upper - upper_terms).astype(jnp.bfloat16)
    lower_masked = masked_panel(l_lower, mask_lower)
    lower_cube = lower_masked.astype(jnp.float32).reshape(ANC, SN, B)
    chosen = jnp.take(x_cube, parent, axis=1)
    link_cube = lp_lower.astype(jnp.float32).reshape(B, SN, B)
    coupling = jnp.einsum("alb,blc->alc", chosen, link_cube, precision=precise).reshape(ANC, SN * B)
    lower_sum = jnp.dot(ancestor, lower_masked.astype(jnp.float32), precision=precise)
    y_lower = (-(lower_sum + coupling)).astype(jnp.bfloat16)
    y_cube = y_lower.astype(jnp.float32).reshape(ANC, SN, B)
    crossed = jnp.einsum("alb,alc->blc", chosen, lower_cube, precision=precise)
    own_terms = jnp.einsum("alb,alc->blc", lower_cube, y_cube, precision=precise)
    parent_diag = jnp.take(diag_upper.astype(jnp.float32).reshape(B, SN, B), parent, axis=1)
    parent_terms = jnp.einsum("blc,cld->bld", parent_diag, link_cube, precision=precise)
    y_parent = (-(crossed + parent_terms)).astype(jnp.bfloat16)
    parent_cube = y_parent.astype(jnp.float32)
    back_terms = jnp.einsum("clb,cld->bld", link_cube, parent_cube, precision=precise)
    diag_lower = (dinv_lower.reshape(B, SN, B) - own_terms - back_terms).astype(jnp.bfloat16)
    return (
        x_upper,
        diag_upper,
        y_lower,
        y_parent.reshape(B, SN * B),
        diag_lower.reshape(B, SN * B),
    )


def solution(mesh):
    return reference
```

profile of v0, /device:TPU:1, one launch (start us, length us, event | category | flops | bytes accessed | tf_op | source)
XLA Modules:
  0.0 620.8 jit_solution(16391168915384105206)
XLA Ops:
  7.2 1.4 dynamic-slice.1
  8.6 1.2 dynamic-slice
  9.9 2.1 compare_bitcast_fusion.1
  11.9 1.1 bitcast_select_fusion.1
  13.0 4.6 collective-permute-start
  17.6 8.2 %collective-permute-done = bf16[768,256]{1,0:T(8,128)(2,1)S(1)} collective-permute-done((bf16[768,256]{1,0:T(8,128)(2,1)S(1)}, bf16[768,256]{1,0:T(8,128)(2,1)S(1)}, u32[]{:S(2)}, u32[]{:S(2)}) %collective-permute-start) | collective-permute-done | bytes 393248 | tf_op jit(solution)/jit(_where)/select_n | solution.py:13
  26.6 81.3 %all-gather.13.cloned.1.call-done = bf16[12288,256]{1,0:T(8,128)(2,1)} async-done(((bf16[768,256]{1,0:T(8,128)(2,1)}), bf16[12288,256]{1,0:T(8,128)(2,1)}) %all-gather.13.cloned.1.call-update) | async-done | bytes 6291472 | tf_op jit(solution)/dot_general | solution.py:22
  107.9 6.4 %copy.9 = bf16[2,8,768,256]{3,1,2,0:T(8,128)(2,1)S(1)} copy(bf16[2,8,768,256]{3,2,1,0:T(8,128)(2,1)} %bitcast.118) | data formatting | bytes 12582912 | tf_op jit(solution)/dot_general | solution.py:22
  114.2 2.7 copy.22
  117.0 7.0 %fusion.38 = f32[2048,768]{1,0:T(8,128)} fusion(bf16[1536,2048]{1,0:T(8,128)(2,1)S(1)} %bitcast.119, bf16[768,1536]{1,0:T(8,128)(2,1)S(1)} %copy-done), kind=kOutput, calls=%fused_computation.53 | convolution fusion | flops 4831838208 | bytes 14942208 | tf_op jit(solution)/dot_general | solution.py:22
  124.1 2.1 compare_bitcast_fusion
  126.3 2.4 collective-permute-start.1
  128.7 22.5 %collective-permute-done.1 = bf16[768,256]{1,0:T(8,128)(2,1)S(1)} collective-permute-done((bf16[768,256]{1,0:T(8,128)(2,1)S(1)}, bf16[768,256]{1,0:T(8,128)(2,1)S(1)}, u32[]{:S(2)}, u32[]{:S(2)}) %collective-permute-start.1) | collective-permute-done | bytes 393248 | tf_op jit(solution)/jit(_where)/select_n | solution.py:13
  151.9 57.5 %reduce-scatter.7.cloned.1.call-done = f32[256,768]{1,0:T(8,128)} async-done(((f32[2048,768]{1,0:T(8,128)}), f32[256,768]{1,0:T(8,128)}) %reduce-scatter.7.cloned.1.call-update) | async-done | bytes 786448
  209.5 2.2 fusion.36
  211.9 65.0 %all-gather.15.cloned.1.call-done = bf16[12288,256]{1,0:T(8,128)(2,1)} async-done(((bf16[768,256]{1,0:T(8,128)(2,1)}), bf16[12288,256]{1,0:T(8,128)(2,1)}) %all-gather.15.cloned.1.call-update) | async-done | bytes 6291472 | tf_op jit(solution)/dot_general | solution.py:36
  276.9 6.4 %copy.11 = bf16[2,8,768,256]{3,1,2,0:T(8,128)(2,1)S(1)} copy(bf16[2,8,768,256]{3,2,1,0:T(8,128)(2,1)} %bitcast.117) | data formatting | bytes 12582912 | tf_op jit(solution)/dot_general | solution.py:36
  283.3 2.7 copy.23
  286.1 7.0 %fusion.39 = f32[2048,768]{1,0:T(8,128)} fusion(bf16[1536,2048]{1,0:T(8,128)(2,1)S(1)} %bitcast.120, bf16[768,1536]{1,0:T(8,128)(2,1)S(1)} %copy-done), kind=kOutput, calls=%fused_computation.54 | convolution fusion | flops 4831838208 | bytes 14942208 | tf_op jit(solution)/dot_general | solution.py:36
  297.7 1.1 convolution_bitcast_fusion.2
  298.8 48.9 %all-gather.17.cloned.1.call-done = f32[768,2048]{0,1:T(8,128)} async-done(((f32[768,256]{0,1:T(8,128)}), f32[768,2048]{0,1:T(8,128)}) %all-gather.17.cloned.1.call-update) | async-done | bytes 6291472 | tf_op jit(solution)/reshape | solution.py:26
  347.7 2.7 convolution_bitcast_fusion.4
  350.4 71.3 %reduce-scatter.9.cloned.1.call-done = f32[256,768]{1,0:T(8,128)} async-done(((f32[2048,768]{1,0:T(8,128)}), f32[256,768]{1,0:T(8,128)}) %reduce-scatter.9.cloned.1.call-update) | async-done | bytes 786448
  421.8 2.1 fusion.1
  423.8 2.1 convolution_bitcast_fusion
  426.0 1.1 copy.10
  427.1 146.3 %all-reduce.8.cloned.1.call-done = (f32[256,256]{0,1:T(8,128)}, f32[256,1,256]{0,2,1:T(8,128)}, f32[256,1,256]{0,2,1:T(8,128)}) async-done(((f32[256,256]{0,1:T(8,128)}, f32[256,1,256]{0,2,1:T(8,128)}, f32[256,1,256]{0,2,1:T(8,128)}), (f32[256,256]{0,1:T(8,128)}, f32[256,1,256]{0,2,1:T(8,128)}, f32[256,1,256]{0,2,1:T(8,128)})) %all-reduce.8.cloned.1.call-update) | async-done | bytes 786448 | tf_op jit(solution)/aub,auc->buc/dot_general | solution.py:27
  573.4 1.7 fusion.35
  578.1 1.7 copy.16
  579.7 30.2 %all-gather.19.cloned.1.call-done = f32[256,2048]{0,1:T(8,128)} async-done(((f32[256,256]{0,1:T(8,128)}), f32[256,2048]{0,1:T(8,128)}) %all-gather.19.cloned.1.call-update) | async-done | bytes 2097168 | tf_op jit(solution)/reshape | solution.py:41
  610.0 1.3 fusion.7
  612.1 1.1 fusion.8
  (46 shorter events, 8.6 us)
Async XLA Ops:
  7.2 109.8 %copy-start = (bf16[768,1536]{1,0:T(8,128)(2,1)S(1)}, bf16[768,1536]{1,0:T(8,128)(2,1)}, u32[]{:S(2)}) copy-start(bf16[768,1536]{1,0:T(8,128)(2,1)} %param.2) | copy-start | bytes 7077892
  7.2 100.7 %all-gather.13.cloned.1.call-start = ((), (), s32[]{:S(2)}) async-start(), calls=%async_computation.2 | async-start | bytes 6684672 | tf_op jit(solution)/dot_general | solution.py:22
  13.0 12.7 %collective-permute-start = (bf16[768,256]{1,0:T(8,128)(2,1)S(1)}, bf16[768,256]{1,0:T(8,128)(2,1)S(1)}, u32[]{:S(2)}, u32[]{:S(2)}) collective-permute-start(bf16[768,256]{1,0:T(8,128)(2,1)S(1)} %bitcast_select_fusion.1), channel_id=1, source_target_pairs={{0,0},{1,16},{2,32},{3,48},{4,64},{5,80},{6,96},{7,112},{8,8},{9,2... | collective-permute-start | bytes 1179656 | tf_op jit(solution)/jit(_where)/select_n | solution.py:13
  25.8 0.7 copy-start.7
  26.5 182.9 %reduce-scatter.7.cloned.1.call-start = ((), (), s32[]{:S(2)}) async-start(), calls=%async_computation.6 | async-start | bytes 7077888
  124.0 2.2 copy-start.3
  124.0 152.9 %all-gather.15.cloned.1.call-start = ((), (), s32[]{:S(2)}) async-start(), calls=%async_computation.3 | async-start | bytes 6684672 | tf_op jit(solution)/dot_general | solution.py:36
  126.3 24.8 %collective-permute-start.1 = (bf16[768,256]{1,0:T(8,128)(2,1)S(1)}, bf16[768,256]{1,0:T(8,128)(2,1)S(1)}, u32[]{:S(2)}, u32[]{:S(2)}) collective-permute-start(bf16[768,256]{1,0:T(8,128)(2,1)S(1)} %bitcast_select_fusion), channel_id=5, source_target_pairs={{0,0},{1,16},{2,32},{3,48},{4,64},{5,80},{6,96},{7,112},{8,8},{9,2... | collective-permute-start | bytes 1179656 | tf_op jit(solution)/jit(_where)/select_n | solution.py:13
  151.1 0.7 copy-start.6
  151.9 195.8 %all-gather.17.cloned.1.call-start = ((), (), s32[]{:S(2)}) async-start(), calls=%async_computation.4 | async-start | bytes 7077888 | tf_op jit(solution)/reshape | solution.py:26
  211.7 210.1 %reduce-scatter.9.cloned.1.call-start = ((), (), s32[]{:S(2)}) async-start(), calls=%async_computation.7 | async-start | bytes 7077888
  293.1 0.7 copy-start.9
  293.1 1.9 copy-start.8
  293.1 4.6 copy-start.1
  293.1 4.6 copy-start.2
  293.1 280.3 %all-reduce.8.cloned.1.call-start = ((), (), s32[]{:S(2)}) async-start(), calls=%async_computation.8 | async-start | bytes 1572864 | tf_op jit(solution)/aub,auc->buc/dot_general | solution.py:27
  298.8 277.4 %copy-start.4 = (bf16[768,256]{0,1:T(8,128)(2,1)S(1)}, bf16[768,256]{0,1:T(8,128)(2,1)}, u32[]{:S(2)}) copy-start(bf16[768,256]{0,1:T(8,128)(2,1)} %get-tuple-element.38) | copy-start | bytes 1179652
  298.8 311.2 %copy-start.5 = (bf16[256,256]{1,0:T(8,128)(2,1)S(1)}, bf16[256,256]{1,0:T(8,128)(2,1)}, u32[]{:S(2)}) copy-start(bf16[256,256]{1,0:T(8,128)(2,1)} %param.7) | copy-start | bytes 393220
  425.9 184.0 %all-gather.19.cloned.1.call-start = ((), (), s32[]{:S(2)}) async-start(), calls=%async_computation.5 | async-start | bytes 2359296 | tf_op jit(solution)/reshape | solution.py:41
Sparse Core Ops, SparseCore 0:
  26.6 81.1 all-gather.12
  124.2 85.2 reduce-scatter.6
  212.5 64.3 all-gather.14
  278.4 69.2 all-gather.16
  350.0 71.7 reduce-scatter.8
  426.0 147.3 all-reduce.7
  575.3 34.6 all-gather.18
where the time goes:
time: 626 us; the launch traced here: 621 us
  waiting for transfers between devices  531 us (85%)
  local copies, waits for them, and re-layouts  31.5 us (5%)
  matrix products  24.4 us (4%)
  between operations  16.9 us (3%)
  other arithmetic  9.29 us (1%)
  starting transfers between devices  7.42 us (1%)
    dot_general x1, waiting for transfers between devices, reference(): jnp.einsum('aub,auc->buc', upper_cube, x_cube, precision=precise)  146 us
    unnamed x9, waiting for transfers between devices  129 us
    dot_general x1, waiting for transfers between devices, reference(): jnp.dot(ancestor, upper_masked.astype(jnp.float32), precision=precise)  81.3 us
    dot_general x1, waiting for transfers between devices, reference(): jnp.dot(ancestor, lower_masked.astype(jnp.float32), precision=precise)  65 us
    reshape x1, waiting for transfers between devices, reference(): x_cube = x_upper.astype(jnp.float32).reshape(ANC, SN, B)  48.9 us
    select_n x2, waiting for transfers between devices, masked_panel(): jnp.where(keeping, shaped, jnp.zeros((), factor.dtype))  30.6 us
    reshape x1, waiting for transfers between devices, reference(): diag_upper.astype(jnp.float32).reshape(B, SN, B)  30.2 us
    unnamed x29, local copies, waits for them, and re-layouts  14.8 us
  transfers between devices with their start and end apart: 9, of which 9 were waited for; matrix products, arithmetic and copies ran while one was open for 5% of the time, Pallas kernels for 0%

commit v1 on v0

v1 whole, which is shorter than its diff:
```python
import functools

import jax
import jax.numpy as jnp
from jax import lax
from jax.experimental import pallas as pl
from jax.experimental.pallas import tpu as pltpu
from jax.sharding import PartitionSpec as P

B = 256
H = 128
MESH = pl.DeviceIdType.MESH
F32 = jnp.float32
BF16 = jnp.bfloat16


def place():
    g, row, col = lax.axis_index("grp"), lax.axis_index("row"), lax.axis_index("col")
    return g, row, col, row // 2, row % 2, col // 4, col % 4


def device(g, x, h, b, z):
    return (g, z * 2 + h, b * 4 + x)


def remote(src, dst, send, recv, target):
    return pltpu.make_async_remote_copy(
        src_ref=src, dst_ref=dst, send_sem=send, recv_sem=recv, device_id=target, device_id_type=MESH
    )


def main_kernel(
    lh, a_hbm, out, a_own, a_oth, s1, panel, part, r1, r2, kept, yb,
    a_sem, as_sem, ar_sem, s1s, s1r, s2s, s2r, ags, agr, p1s, p1r, p2s, p2r, p3s, p3r,
):
    g, row, col, z, h, b, x = place()
    rows = a_own.shape[0]
    quarter, sl, half = rows // 4, rows // 8, rows // 2
    chunks = panel.shape[0]

    local_a = pltpu.make_async_copy(a_hbm, a_own, a_sem)
    local_a.start()
    other = (1 - g, row, col)
    swap_a = remote(a_hbm, a_oth, as_sem, ar_sem, other)

    def first(pn, dz, dg):
        gt, zt = (g + dg) % 2, (z + dz) % 4
        return remote(
            lh.at[gt, pn, zt], s1.at[g, z, pn], s1s.at[pn, dg * 4 + dz], s1r.at[pn, g * 4 + z],
            device(gt, x, h, b, zt),
        )

    def first_in(pn, dz, dg):
        gs, zs = (g + dg) % 2, (z + dz) % 4
        return gs, zs, remote(
            lh.at[g, pn, z], s1.at[gs, zs, pn], s1s.at[pn, 0], s1r.at[pn, gs * 4 + zs], device(g, x, h, b, z)
        )

    order = [(dz, dg) for dz in (2, 1, 3, 0) for dg in (0, 1)]
    for pn in range(2):
        for dz, dg in order:
            if (dz, dg) != (0, 0):
                first(pn, dz, dg).start()
        s1[g, z, pn] = lh[g, pn, z]
        if pn == 0:
            swap_a.start()

    def second(pn, dx, dg, dh):
        zs, gs, ht = (x + dx) % 4, (b + dg) % 2, (h + dh) % 2
        spot = panel.at[
            pn * 4 + col // 2,
            pl.ds(pl.multiple_of(h * rows + z * quarter, 16), quarter),
            pl.ds(pl.multiple_of((col % 2) * H, H), H),
        ]
        return zs, gs, remote(
            s1.at[gs, zs, pn], spot, s2s.at[pn, dx * 4 + dg * 2 + dh], s2r.at[pn, h * 8 + col],
            device(g, zs, ht, gs, z),
        )

    for pn in range(2):
        for dz, dg in order:
            if (dz, dg) != (0, 0):
                first_in(pn, dz, dg)[2].wait_recv()
        for dx in (2, 1, 3, 0):
            for dg in range(2):
                for dh in range(2):
                    zs, gs, copy = second(pn, dx, dg, dh)
                    if (dx, dg, dh) != (0, 0, 0):
                        copy.start()
                    else:
                        panel[
                            pn * 4 + col // 2,
                            pl.ds(pl.multiple_of(h * rows + z * quarter, 16), quarter),
                            pl.ds(pl.multiple_of((col % 2) * H, H), H),
                        ] = s1[gs, zs, pn]

    def second_in(m, e, hs):
        cs = (m % 4) * 2 + e
        spot = panel.at[
            m, pl.ds(pl.multiple_of(hs * rows + z * quarter, 16), quarter), pl.ds(e * H, H)
        ]
        pn = m // 4
        return cs, remote(
            s1.at[0, 0, 0], spot, s2s.at[pn, 0], s2r.at[pn, hs * 8 + cs], device(g, x, h, b, z)
        )

    right = device(g, x, h, b, (z + 1) % 4)
    left = device(g, x, h, b, (z + 3) % 4)

    def spot_of(m, hs, q):
        return panel.at[m, pl.ds(pl.multiple_of(hs * rows + q * quarter, 16), quarter)]

    def gather(m, slot, q, hs, to):
        return remote(spot_of(m, hs, q), spot_of(m, hs, q), ags.at[m, slot], agr.at[m, slot], to)

    def step_a(m):
        for hs in range(2):
            for e in range(2):
                cs, copy = second_in(m, e, hs)

                @pl.when(jnp.logical_not((cs == col) & (hs == h)))
                def _():
                    copy.wait_recv()

        for hs in range(2):
            gather(m, hs, z, hs, right).start()
            gather(m, 2 + hs, z, hs, left).start()

    def step_b(m):
        gather(m, 0, (z + 3) % 4, 0, right).wait_recv()
        gather(m, 4, (z + 3) % 4, 0, right).start()
        gather(m, 3, (z + 1) % 4, 1, left).wait_recv()
        gather(m, 5, (z + 1) % 4, 1, left).start()

    xr = device(g, (x + 1) % 4, h, b, z)
    xl = device(g, (x + 3) % 4, h, b, z)
    far = (x + 2) % 4

    def half_copy(m, way):
        return remote(
            part.at[m, far, way], r1.at[m, way], p1s.at[m, way], p1r.at[m, way], xr if way == 0 else xl
        )

    def full_copy(m, way):
        near = (x + 1) % 4 if way == 0 else (x + 3) % 4
        return remote(
            part.at[m, near], r2.at[m, way], p2s.at[m, way], p2r.at[m, way], xr if way == 0 else xl
        )

    def pair_copy(m):
        return remote(
            r2.at[m, 0, :, 1 - b], yb.at[m], p3s.at[m], p3r.at[m], device(g, x, h, 1 - b, z)
        )

    def step_c(m):
        gather(m, 1, (z + 3) % 4, 1, right).wait_recv()
        gather(m, 2, (z + 1) % 4, 0, left).wait_recv()
        gather(m, 4, far_z, 0, right).wait_recv()
        gather(m, 5, far_z, 1, left).wait_recv()
        for o, a in enumerate((a_own, a_oth)):
            for bt in range(2):
                product = jnp.dot(
                    a[bt * half:(bt + 1) * half, :], panel[m], preferred_element_type=F32
                ).astype(BF16)
                for xt in range(4):
                    part[m, xt, o, bt] = product[xt * sl:(xt + 1) * sl]
        half_copy(m, 0).start()
        half_copy(m, 1).start()

    def step_d(m):
        for way in range(2):
            near = (x + 1) % 4 if way == 0 else (x + 3) % 4
            half_copy(m, way).wait_recv()
            part[m, near, way] = (part[m, near, way].astype(F32) + r1[m, way].astype(F32)).astype(BF16)
            full_copy(m, way).start()

    def step_e(m):
        full_copy(m, 0).wait_recv()
        full_copy(m, 1).wait_recv()
        for bt in range(2):
            total = (
                part[m, x, :, bt].astype(F32) + r2[m, 0, :, bt].astype(F32) + r2[m, 1, :, bt].astype(F32)
            )
            r2[m, 0, :, bt] = total.astype(BF16)

            @pl.when(b == bt)
            def _():
                kept[m] = total

        pair_copy(m).start()

    def step_f(m):
        pair_copy(m).wait_recv()
        total = -(kept[m] + yb[m].astype(F32))
        result = total.astype(BF16)
        out[2 * m] = result[:, :, :H]
        out[2 * m + 1] = result[:, :, H:]

    far_z = (z + 2) % 4
    local_a.wait()
    swap_a.wait_recv()

    steps = (step_a, step_b, step_c, step_d, step_e, step_f)

    def body(t, carry):
        for k, step in enumerate(steps):
            m = t - k

            @pl.when((m >= 0) & (m < chunks))
            def _(step=step, m=m):
                step(m)

        return carry

    lax.fori_loop(0, chunks + len(steps) - 1, body, 0)

    swap_a.wait_send()
    for pn in range(2):
        for dz, dg in order:
            if (dz, dg) != (0, 0):
                first(pn, dz, dg).wait_send()
        for dx in range(4):
            for dg in range(2):
                for dh in range(2):
                    if (dx, dg, dh) != (0, 0, 0):
                        second(pn, dx, dg, dh)[2].wait_send()

    def drain(m, carry):
        for hs in range(2):
            gather(m, hs, z, hs, right).wait_send()
            gather(m, 2 + hs, z, hs, left).wait_send()
        gather(m, 4, z, 0, right).wait_send()
        gather(m, 5, z, 1, left).wait_send()
        for way in range(2):
            half_copy(m, way).wait_send()
            full_copy(m, way).wait_send()
        pair_copy(m).wait_send()
        return carry

    lax.fori_loop(0, chunks, drain, 0)


def main_call(lh, a):
    rows, depth = a.shape
    quarter, sl = rows // 4, rows // 8
    chunks = 8
    dma = pltpu.SemaphoreType.DMA
    return pl.pallas_call(
        main_kernel,
        out_shape=jax.ShapeDtypeStruct((16, 2, sl, H), BF16),
        in_specs=[pl.BlockSpec(memory_space=pltpu.VMEM), pl.BlockSpec(memory_space=pl.ANY)],
        out_specs=pl.BlockSpec(memory_space=pltpu.VMEM),
        scratch_shapes=[
            pltpu.VMEM((rows, depth), BF16),
            pltpu.VMEM((rows, depth), BF16),
            pltpu.VMEM((2, 4, 2, quarter, H), BF16),
            pltpu.VMEM((chunks, depth, B), BF16),
            pltpu.VMEM((chunks, 4, 2, 2, sl, B), BF16),
            pltpu.VMEM((chunks, 2, 2, sl, B), BF16),
            pltpu.VMEM((chunks, 2, 2, 2, sl, B), BF16),
            pltpu.VMEM((chunks, 2, sl, B), F32),
            pltpu.VMEM((chunks, 2, sl, B), BF16),
            dma, dma, dma,
            dma((2, 8)), dma((2, 8)),
            dma((2, 16)), dma((2, 16)),
            dma((chunks, 6)), dma((chunks, 6)),
            dma((chunks, 2)), dma((chunks, 2)),
            dma((chunks, 2)), dma((chunks, 2)),
            dma((chunks,)), dma((chunks,)),
        ],
        compiler_params=pltpu.CompilerParams(has_side_effects=True, vmem_limit_bytes=60 * 2**20),
        name="panels",
    )(lh, a)


def tail_kernel(
    parent, slices, mu, ml, lp, du_in, dl_in,
    x_out, y_out, du_out, yp_out, dl_out,
    chosen_s, xt, ct, st, red_s, red, dcol, back,
    ts, tr, rs, rr, cs, cr, gs, gr,
):
    g, row, col, z, h, b, x = place()
    me = g * 8 + row
    sl = slices.shape[2]
    n_r, n_c = 16, 8
    deep = B // n_r

    for c in range(n_c):
        chosen_s[c] = slices[parent[c]]

    mine = pl.ds(pl.multiple_of(col * sl, 16), sl)
    lanes = pl.ds(pl.multiple_of(g * H, H), H)
    kinds = (xt, ct, st)

    def source(k, c, o):
        if k == 0:
            return slices.at[c, o]
        if k == 1:
            return chosen_s.at[c, o]
        return slices.at[8 + c, o]

    def turn(k, i):
        dc, o = i // 2, i % 2
        c = (col + dc) % n_c
        return remote(
            source(k, c, o), kinds[k].at[mine, lanes], ts.at[k, i], tr.at[k, g * 8 + col],
            ((g + o) % 2, row, c),
        )

    def turn_in(k, i):
        dc, o = i // 2, i % 2
        c, gg = (col + dc) % n_c, (g + o) % 2
        return remote(
            source(k, 0, 0),
            kinds[k].at[pl.ds(pl.multiple_of(c * sl, 16), sl), pl.ds(pl.multiple_of(gg * H, H), H)],
            ts.at[k, 0], tr.at[k, gg * 8 + c], (g, row, col),
        )

    def loop(lo, hi, f):
        def body(i, carry):
            f(i)
            return carry

        lax.fori_loop(lo, hi, body, 0)

    for k in range(3):
        loop(1, 16, lambda i, k=k: turn(k, i).start())
    xt[mine, lanes] = slices[col, 0]
    ct[mine, lanes] = chosen_s[col, 0]
    st[mine, lanes] = slices[8 + col, 0]

    def peer(d):
        r = (me + d) % n_r
        return r, (r // 8, r % 8, col)

    def scatter(k, d):
        r, to = peer(d)
        return remote(red_s.at[k, r], red.at[k, me], rs.at[k, d], rr.at[k, me], to)

    def scatter_in(k, d):
        r, _ = peer(d)
        return remote(red_s.at[k, r], red.at[k, r], rs.at[k, d], rr.at[k, r], (g, row, col))

    def reduce_start(k, value):
        red_s[k] = value.reshape(n_r, deep, B).astype(BF16)
        loop(1, n_r, lambda d: scatter(k, d).start())
        red[k, me] = red_s[k, me]

    def reduce_end(k):
        loop(1, n_r, lambda d: scatter_in(k, d).wait_recv())
        return jnp.sum(red[k].astype(F32), axis=0)

    outs = (du_out, yp_out, dl_out)

    def spread(k, d):
        r, to = peer(d)
        return remote(outs[k].at[me], outs[k].at[me], gs.at[k, d], gr.at[k, me], to)

    def spread_in(k, d):
        r, _ = peer(d)
        return remote(outs[k].at[r], outs[k].at[r], gs.at[k, d], gr.at[k, r], (g, row, col))

    def flipped(p, q):
        return lax.dot_general(p, q, (((0,), (0,)), ((), ())), preferred_element_type=F32)

    loop(1, 16, lambda i: turn_in(0, i).wait_recv())
    x_out[...] = xt[...]
    reduce_start(0, flipped(mu[...], xt[...]))
    loop(1, 16, lambda i: turn_in(1, i).wait_recv())
    reduce_start(1, flipped(ct[...], ml[...]))
    loop(1, 16, lambda i: turn_in(2, i).wait_recv())
    y = (st[...].astype(F32) - jnp.dot(ct[...], lp[...], preferred_element_type=F32)).astype(BF16)
    y_out[...] = y
    reduce_start(2, flipped(ml[...], y))

    du = (du_in[me] - reduce_end(0)).astype(BF16)
    du_out[me] = du
    dcol[col] = du
    loop(1, n_r, lambda d: spread(0, d).start())

    def column(d):
        c = (col + d) % n_c
        return remote(dcol.at[col], dcol.at[col], cs.at[d], cr.at[col], (g, row, c))

    def column_in(d):
        c = (col + d) % n_c
        return remote(dcol.at[c], dcol.at[c], cs.at[d], cr.at[c], (g, row, col))

    loop(1, n_c, lambda d: column(d).start())
    crossed = reduce_end(1)
    loop(1, n_c, lambda d: column_in(d).wait_recv())
    own = dcol[parent[col]]
    yp_out[me] = (-(crossed + jnp.dot(own, lp[...], preferred_element_type=F32))).astype(BF16)
    loop(1, n_r, lambda d: spread(1, d).start())
    lower = dl_in[me] - reduce_end(2)
    loop(1, n_r, lambda d: spread_in(1, d).wait_recv())
    back[...] = flipped(lp[...], yp_out[...].reshape(B, B)).reshape(n_r, deep, B)
    dl_out[me] = (lower - back[me]).astype(BF16)
    loop(1, n_r, lambda d: spread(2, d).start())
    loop(1, n_r, lambda d: spread_in(0, d).wait_recv())
    loop(1, n_r, lambda d: spread_in(2, d).wait_recv())

    for k in range(3):
        loop(1, 16, lambda i, k=k: turn(k, i).wait_send())
        loop(1, n_r, lambda d, k=k: scatter(k, d).wait_send())
        loop(1, n_r, lambda d, k=k: spread(k, d).wait_send())
    loop(1, n_c, lambda d: column(d).wait_send())


def tail_call(parent, slices, mu, ml, lp, du, dl):
    rows = mu.shape[0]
    dma = pltpu.SemaphoreType.DMA
    vmem = pl.BlockSpec(memory_space=pltpu.VMEM)
    deep = B // 16
    block = jax.ShapeDtypeStruct((rows, B), BF16)
    square = jax.ShapeDtypeStruct((16, deep, B), BF16)
    x, y, d_u, y_p, d_l = pl.pallas_call(
        tail_kernel,
        out_shape=(block, block, square, square, square),
        in_specs=[pl.BlockSpec(memory_space=pltpu.SMEM)] + [vmem] * 6,
        out_specs=(vmem,) * 5,
        scratch_shapes=[
            pltpu.VMEM((8,) + slices.shape[1:], BF16),
            pltpu.VMEM((rows, B), BF16),
            pltpu.VMEM((rows, B), BF16),
            pltpu.VMEM((rows, B), BF16),
            pltpu.VMEM((3, 16, deep, B), BF16),
            pltpu.VMEM((3, 16, deep, B), BF16),
            pltpu.VMEM((8, deep, B), BF16),
            pltpu.VMEM((16, deep, B), F32),
            dma((3, 16)), dma((3, 16)),
            dma((3, 16)), dma((3, 16)),
            dma((8,)), dma((8,)),
            dma((3, 16)), dma((3, 16)),
        ],
        compiler_params=pltpu.CompilerParams(has_side_effects=True, vmem_limit_bytes=40 * 2**20),
        name="tail",
    )(parent, slices, mu, ml, lp, du.reshape(16, deep, B), dl.reshape(16, deep, B))
    return x, d_u.reshape(B, B), y, y_p.reshape(B, B), d_l.reshape(B, B)


def step(a, lu, mask_u, du, ll, mask_l, parent, lp, dl):
    g, row, col = lax.axis_index("grp"), lax.axis_index("row"), lax.axis_index("col")
    rows = a.shape[0]
    blocks = max(rows // B, 1)
    base = (g * 8 + row) * rows

    def masked(factor, mask):
        line = lax.dynamic_slice(mask, (col, 0), (1, mask.shape[1]))[0]
        keep = line[(base + jnp.arange(rows)) // B]
        return jnp.where(keep[:, None] > 0, factor, jnp.zeros((), factor.dtype))

    mu, ml = masked(lu, mask_u), masked(ll, mask_l)
    both = jnp.stack([mu, ml]).reshape(2, 4, rows // 4, 2, H)
    lh = jnp.transpose(both, (3, 0, 1, 2, 4))
    slices = main_call(lh, a)
    return tail_call(parent, slices, mu, ml, lp, du, dl)


def solution(mesh):
    rows, cols = P(("grp", "row"), "col"), P(None, "col")
    none = P(None, None)
    return jax.shard_map(
        step,
        mesh=mesh,
        in_specs=(rows, rows, none, cols, rows, none, P(None), cols, cols),
        out_specs=(rows, cols, rows, cols, cols),
        check_vma=False,
    )
```

time: 626 us -> 238 us (0.38)
  waiting for transfers between devices: 531 us -> 0 us
  Pallas kernels: 0 us -> 161 us
  other arithmetic: 9.29 us -> 64.4 us
  matrix products: 24.4 us -> 0 us
  local copies, waits for them, and re-layouts: 31.5 us -> 10.6 us
  between operations: 16.9 us -> 0.86 us
  starting transfers between devices: 7.42 us -> 0 us
    dot_general x3 -> x0, waiting for transfers between devices: 293 us -> none  [the longest x1 146 us: reference(): jnp.einsum('aub,auc->buc', upper_cube, x_cube, precision=precise)]
    pallas_call x0 -> x2, Pallas kernels: none -> 161 us  [the longest x1 110 us: main_call(): pl.pallas_call(main_kernel, out_shape=jax.ShapeDtypeStruct((16, 2, sl, H)...]
    unnamed x9 -> x0, waiting for transfers between devices: 129 us -> none
    reshape x2 -> x0, waiting for transfers between devices: 79.1 us -> none  [the longest x1 48.9 us: reference(): x_cube = x_upper.astype(jnp.float32).reshape(ANC, SN, B)]
    gt x2, other arithmetic: 4.16 us -> 51.2 us  [masked(): return jnp.where(keep[:, None] > 0, factor, jnp.zeros((), factor.dtype))]
    select_n x2 -> x0, waiting for transfers between devices: 30.6 us -> none  [masked_panel(): jnp.where(keeping, shaped, jnp.zeros((), factor.dtype))]
    dot_general x8 -> x0, matrix products: 24.4 us -> none  [the longest x1 7.01 us: reference(): jnp.dot(ancestor, lower_masked.astype(jnp.float32), precision=precise)]
    dot_general x2 -> x0, local copies, waits for them, and re-layouts: 12.7 us -> none  [the longest x1 6.36 us: reference(): jnp.dot(ancestor, upper_masked.astype(jnp.float32), precision=precise)]
  transfers between devices with their start and end apart: 9 -> 0, of which waited for: 9 -> 0; matrix products, arithmetic and copies ran while one was open for 5% -> 0% of each run, Pallas kernels for 0% -> 0%
where the time goes in v1:
time: 238 us; the launch traced here: 237 us
  Pallas kernels  161 us (68%)
  other arithmetic  64.4 us (27%)
  local copies, waits for them, and re-layouts  10.6 us (4%)
    pallas_call x1, Pallas kernels, main_call(): pl.pallas_call(main_kernel, out_shape=jax.ShapeDtypeStruct((16, 2, sl, H)...  110 us
    gt x2, other arithmetic, masked(): return jnp.where(keep[:, None] > 0, factor, jnp.zeros((), factor.dtype))  51.2 us
    pallas_call x1, Pallas kernels, tail_call(): pl.pallas_call(tail_kernel, out_shape=(block, block, square, square, squa...  51.1 us
    gather x22, other arithmetic, masked(): keep = line[(base + jnp.arange(rows)) // B]  9.88 us
    unnamed x17, local copies, waits for them, and re-layouts  5.29 us

profile of v1, /device:TPU:1, one launch (start us, length us, event | category | flops | bytes accessed | tf_op | source)
XLA Modules:
  0.0 236.5 jit_solution(3755021780202174416)
XLA Ops:
  0.6 0.0 copy-start
  0.7 0.7 copy-done
  1.3 0.7 constant_dynamic-slice_fusion
  3.1 0.7 fusion.7
  3.8 0.7 fusion.4
  4.4 0.7 fusion.6
  5.2 0.7 fusion.5
  5.9 0.7 fusion.3
  6.6 0.7 fusion.2
  7.4 8.9 %fusion = (s32[768]{0:T(1024)S(1)}, s32[768]{0:T(1024)S(1)}) fusion(s32[]{:T(128)} %bitcast.89, s32[]{:T(128)} %bitcast.90, s32[]{:T(128)} %bitcast.91, s32[]{:T(128)} %bitcast.92, s32[]{:T(128)} %bitcast.93, s32[]{:T(128)} %bitcast.95, s32[]{:T(128)} %bitcast.94, s32[]{:T(128)S(6)} %mul.7, s32[]{:T(128)} %bitcast.47, s32[]{:T(128)} %bitcast.46, ...), kind=kLoop, calls=%fused_computation.63 | loop fusion | flops 28416 | bytes 6204 | tf_op jit(solution)/shard_map/gather | solution.py:450
  16.2 25.5 %select_compare_fusion.1 = pred[768]{0:T(1024)(128)(4,1)S(1)} fusion(pred[768]{0:T(1024)(128)(4,1)S(1)} %get-tuple-element.111, pred[768]{0:T(1024)(128)(4,1)S(1)} %get-tuple-element.112, pred[768]{0:T(1024)(128)(4,1)S(1)} %get-tuple-element.113, pred[768]{0:T(1024)(128)(4,1)S(1)} %get-tuple-element.114, pred[768]{0:T(1024)(128)(4,1)S(1)} %get-tuple-element.115, ...), kind=kLoop, calls=%fused_computation.62 | loop fusion | flops 32256 | bytes 35492 | tf_op jit(solution)/shard_map/gt | solution.py:451
  41.8 25.7 %select_compare_fusion = pred[768]{0:T(1024)(128)(4,1)S(1)} fusion(pred[768]{0:T(1024)(128)(4,1)S(1)} %get-tuple-element.111, pred[768]{0:T(1024)(128)(4,1)S(1)} %get-tuple-element.112, pred[768]{0:T(1024)(128)(4,1)S(1)} %get-tuple-element.113, pred[768]{0:T(1024)(128)(4,1)S(1)} %get-tuple-element.114, pred[768]{0:T(1024)(128)(4,1)S(1)} %get-tuple-element.115, ...), kind=kLoop, calls=%fused_computation.61 | loop fusion | flops 32256 | bytes 35492 | tf_op jit(solution)/shard_map/gt | solution.py:451
  67.5 1.2 broadcast_select_fusion.ml
  68.6 1.2 broadcast_select_fusion.1.mu
  69.8 0.1 stack.9
  69.9 0.1 copy.16
  70.0 0.1 stack.10
  70.1 0.1 copy.17
  70.1 0.0 copy-start.2
  70.2 0.0 copy-start.3
  70.2 0.0 copy-start.4
  70.2 0.0 copy-start.5
  70.2 0.9 maximum_bitcast_fusion.lh
  71.1 109.6 %panels.1.slices = bf16[16,2,96,128]{3,2,1,0:T(8,128)(2,1)} custom-call(bf16[2,2,4,192,128]{4,3,2,1,0:T(8,128)(2,1)} %maximum_bitcast_fusion.lh, bf16[768,1536]{1,0:T(8,128)(2,1)} %a_hbm.1), custom_call_target="tpu_custom_call" | custom-call | tf_op jit(solution)/shard_map/panels/pallas_call | solution.py:248
  180.8 0.0 copy-done.2
  180.8 1.1 copy-done.1
  181.9 51.1 %tail.1 = (bf16[768,256]{1,0:T(8,128)(2,1)S(1)}, bf16[768,256]{1,0:T(8,128)(2,1)S(1)}, bf16[16,16,256]{2,1,0:T(8,128)(2,1)S(1)}, bf16[16,16,256]{2,1,0:T(8,128)(2,1)S(1)}, bf16[16,16,256]{2,1,0:T(8,128)(2,1)S(1)}) custom-call(s32[8]{0:T(128)S(1)} %copy-done.5, bf16[16,2,96,128]{3,2,1,0:T(8,128)(2,1)S(1)} %copy-done.1, ...), custom_call_target="tpu_custom_call" | custom-call | tf_op jit(solution)/shard_map/tail/pallas_call | solution.py:417
  233.0 0.7 copy.23
  233.8 0.7 copy.24
  234.4 0.7 copy.25
  235.2 0.7 copy.26
  235.8 0.7 copy.27
  (26 shorter events, 1.0 us)
Async XLA Ops:
  0.6 0.7 copy-start
  70.1 110.6 %copy-start.2 = (f32[256,256]{1,0:T(8,128)S(1)}, f32[256,256]{1,0:T(8,128)}, u32[]{:S(2)}) copy-start(f32[256,256]{1,0:T(8,128)} %param.12) | copy-start | bytes 786436
  70.2 110.6 %copy-start.3 = (f32[256,256]{1,0:T(8,128)S(1)}, f32[256,256]{1,0:T(8,128)}, u32[]{:S(2)}) copy-start(f32[256,256]{1,0:T(8,128)} %param.17) | copy-start | bytes 786436
  70.2 110.6 %copy-start.4 = (bf16[256,256]{1,0:T(8,128)(2,1)S(1)}, bf16[256,256]{1,0:T(8,128)(2,1)}, u32[]{:S(2)}) copy-start(bf16[256,256]{1,0:T(8,128)(2,1)} %lp.1) | copy-start | bytes 393220
  70.2 110.6 %copy-start.5 = (s32[8]{0:T(128)S(1)}, s32[8]{0:T(128)}, u32[]{:S(2)}) copy-start(s32[8]{0:T(128)} %parent.1) | copy-start | bytes 100
  180.8 1.1 copy-start.1

commit v2 on v0

v2 whole, which is shorter than its diff:
```python
import jax
import jax.numpy as jnp
from jax import lax
from jax.experimental import pallas as pl
from jax.experimental.pallas import tpu as pltpu
from jax.sharding import PartitionSpec as P

B = 256
H = 128
CH = 8
NS = 16
MESH = pl.DeviceIdType.MESH
F32 = jnp.float32
BF16 = jnp.bfloat16


def device(g, x, h, b, z):
    return (g, z * 2 + h, b * 4 + x)


def remote(src, dst, send, recv, target):
    return pltpu.make_async_remote_copy(
        src_ref=src, dst_ref=dst, send_sem=send, recv_sem=recv, device_id=target, device_id_type=MESH
    )


def aligned(start, size):
    return pl.ds(pl.multiple_of(start, size), size)


def loop(lo, hi, f):
    def body(i, carry):
        f(i)
        return carry

    lax.fori_loop(lo, hi, body, 0)


def flipped(p, q):
    return lax.dot_general(p, q, (((0,), (0,)), ((), ())), preferred_element_type=F32)


def kernel(
    mask_u, mask_l, parent, lu, ll, a_hbm, lp, du_in, dl_in,
    x_out, y_out, du_out, yp_out, dl_out,
    masked, a, s1, panel, part, r1, r2, kept, yb, xs, chosen_s, xst, ct, cl, red_s, red, dcol, back,
    a_sem, as_sem, ar_sem, s1s, s1r, s2s, s2r, ags, agr, p1s, p1r, p2s, p2r, p3s, p3r,
    ts, tr, rs, rr, cs, cr, gs, gr,
):
    g, row, col = lax.axis_index("grp"), lax.axis_index("row"), lax.axis_index("col")
    z, h, b, x = row // 2, row % 2, col // 4, col % 4
    me = g * 8 + row
    rows = a.shape[1]
    quarter, sl, half = rows // 4, rows // 8, rows // 2
    bl = min(B, rows)
    here = (g, row, col)

    for pn, (factor, mask) in enumerate(((lu, mask_u), (ll, mask_l))):
        for i in range(rows // bl):
            keep = mask[col, (me * rows + i * bl) // B] > 0
            values = factor[i * bl:(i + 1) * bl, :]
            masked[pn, i * bl:(i + 1) * bl, :] = jnp.where(keep, values, jnp.zeros_like(values))

    local_a = pltpu.make_async_copy(a_hbm, a.at[0], a_sem)
    local_a.start()
    swap_a = remote(a_hbm, a.at[1], as_sem, ar_sem, (1 - g, row, col))

    def piece(pn, q, half_of):
        return masked.at[pn, aligned(q * quarter, quarter), aligned(half_of * H, H)]

    def first(pn, dz, dg):
        gt, zt = (g + dg) % 2, (z + dz) % 4
        return remote(
            piece(pn, zt, gt), s1.at[g, z, pn], s1s.at[pn, dg * 4 + dz], s1r.at[pn, g * 4 + z],
            device(gt, x, h, b, zt),
        )

    def first_in(pn, dz, dg):
        gf, zf = (g + dg) % 2, (z + dz) % 4
        return remote(piece(pn, z, g), s1.at[gf, zf, pn], s1s.at[pn, 0], s1r.at[pn, gf * 4 + zf], here)

    order = [(dz, dg) for dz in (2, 1, 3, 0) for dg in (0, 1)]
    for pn in range(2):
        for dz, dg in order:
            if (dz, dg) != (0, 0):
                first(pn, dz, dg).start()
        s1[g, z, pn] = masked[pn, aligned(z * quarter, quarter), aligned(g * H, H)]
        if pn == 0:
            swap_a.start()

    def spot_from(pn, hf, cf, lane):
        return (pn * 4 + cf // 2, aligned(hf * rows + z * quarter, quarter), lane)

    def second(pn, dx, dg, dh):
        zf, gf, ht = (x + dx) % 4, (b + dg) % 2, (h + dh) % 2
        return zf, gf, remote(
            s1.at[gf, zf, pn], panel.at[spot_from(pn, h, col, aligned((col % 2) * H, H))],
            s2s.at[pn, dx * 4 + dg * 2 + dh], s2r.at[pn, h * 8 + col], device(g, zf, ht, gf, z),
        )

    far_first = [(dx, dg, dh) for dx in (2, 1, 3, 0) for dg in range(2) for dh in range(2)]
    for pn in range(2):
        for dz, dg in order:
            if (dz, dg) != (0, 0):
                first_in(pn, dz, dg).wait_recv()
        for way in far_first:
            zf, gf, copy = second(pn, *way)
            if way != (0, 0, 0):
                copy.start()
            else:
                panel[spot_from(pn, h, col, aligned((col % 2) * H, H))] = s1[gf, zf, pn]

    right, left = device(g, x, h, b, (z + 1) % 4), device(g, x, h, b, (z + 3) % 4)
    far_z = (z + 2) % 4

    def gather(m, slot, q, hf, to):
        spot = panel.at[m, aligned(hf * rows + q * quarter, quarter)]
        return remote(spot, spot, ags.at[m, slot], agr.at[m, slot], to)

    def step_a(m):
        pn = m // 4
        for hf in range(2):
            for e in range(2):
                cf = (m % 4) * 2 + e
                copy = remote(
                    s1.at[0, 0, 0], panel.at[spot_from(pn, hf, cf, pl.ds(e * H, H))],
                    s2s.at[pn, 0], s2r.at[pn, hf * 8 + cf], here,
                )
                pl.when(jnp.logical_not((cf == col) & (hf == h)))(copy.wait_recv)
        for hf in range(2):
            gather(m, hf, z, hf, right).start()
            gather(m, 2 + (1 - hf), z, 1 - hf, left).start()

    def step_b(m):
        gather(m, 0, (z + 3) % 4, 0, right).wait_recv()
        gather(m, 4, (z + 3) % 4, 0, right).start()
        gather(m, 3, (z + 1) % 4, 1, left).wait_recv()
        gather(m, 5, (z + 1) % 4, 1, left).start()

    def step_w(m):
        gather(m, 1, (z + 3) % 4, 1, right).wait_recv()
        gather(m, 2, (z + 1) % 4, 0, left).wait_recv()
        gather(m, 4, far_z, 0, right).wait_recv()
        gather(m, 5, far_z, 1, left).wait_recv()

    xr, xl = device(g, (x + 1) % 4, h, b, z), device(g, (x + 3) % 4, h, b, z)

    def near(way):
        return (x + 1 + 2 * way) % 4

    def half_copy(n, way):
        return remote(
            part.at[n, (x + 2) % 4, way], r1.at[n, way], p1s.at[n, way], p1r.at[n, way], xl if way else xr
        )

    def full_copy(n, way):
        return remote(
            part.at[n, near(way)], r2.at[n, way], p2s.at[n, way], p2r.at[n, way], xl if way else xr
        )

    def pair_copy(n):
        return remote(r2.at[n, 0, 1 - b], yb.at[n], p3s.at[n], p3r.at[n], device(g, x, h, 1 - b, z))

    def step_c(n):
        m, o = n // 2, n % 2
        for bt in range(2):
            product = jnp.dot(
                a[o, bt * half:(bt + 1) * half, :], panel[m], preferred_element_type=F32
            ).astype(BF16)
            for xt in range(4):
                part[n, xt, bt] = product[xt * sl:(xt + 1) * sl]
        half_copy(n, 0).start()
        half_copy(n, 1).start()

    def step_d(n):
        for way in range(2):
            half_copy(n, way).wait_recv()
            part[n, near(way), way] = (
                part[n, near(way), way].astype(F32) + r1[n, way].astype(F32)
            ).astype(BF16)
        for way in range(2):
            full_copy(n, way).start()

    def step_e(n):
        full_copy(n, 0).wait_recv()
        full_copy(n, 1).wait_recv()
        for bt in range(2):
            total = part[n, x, bt].astype(F32) + r2[n, 0, bt].astype(F32) + r2[n, 1, bt].astype(F32)
            r2[n, 0, bt] = total.astype(BF16)

            @pl.when(b == bt)
            def _():
                kept[n] = total

        pair_copy(n).start()

    mine, lanes = aligned(col * sl, sl), aligned(g * H, H)

    def turn(pn, c, o):
        return remote(
            xs.at[pn * 8 + c, o], xst.at[pn, mine, lanes], ts.at[pn, c * 2 + o], tr.at[pn, g * 8 + col],
            ((g + o) % 2, row, c),
        )

    def wait_turned(dst, k):
        def one(i):
            c, gf = (col + i // 2) % 8, (g + i % 2) % 2
            remote(
                xs.at[0, 0], dst.at[aligned(c * sl, sl), aligned(gf * H, H)], ts.at[k, 0], tr.at[k, gf * 8 + c], here
            ).wait_recv()

        loop(1, 16, one)

    def step_f(n):
        m, o = n // 2, n % 2
        pn = n // 8
        pair_copy(n).wait_recv()
        result = (-(kept[n] + yb[n].astype(F32))).astype(BF16)
        for e in range(2):
            xs[2 * m + e, o] = result[:, e * H:(e + 1) * H]
        for e in range(2):
            c = 2 * (m % 4) + e
            self_turn = (c == col) & (o == 0)
            pl.when(jnp.logical_not(self_turn))(turn(pn, c, o).start)

            @pl.when(self_turn)
            def _():
                xst[pn, mine, lanes] = result[:, e * H:(e + 1) * H]

    def pick(i):
        c, o = (col + i // 2) % 8, i % 2
        return remote(
            chosen_s.at[c, o], ct.at[mine, lanes], ts.at[2, i], tr.at[2, g * 8 + col], ((g + o) % 2, row, c)
        )

    def peer(d):
        r = (me + d) % 16
        return r, (r // 8, r % 8, col)

    def scatter(k, d):
        r, to = peer(d)
        return remote(red_s.at[k, r], red.at[k, me], rs.at[k, d], rr.at[k, me], to)

    def reduce_start(k, value):
        red_s[k] = value.reshape(16, B // 16, B).astype(BF16)
        loop(1, 16, lambda d: scatter(k, d).start())
        red[k, me] = red_s[k, me]

    def reduce_end(k):
        def one(d):
            r, _ = peer(d)
            remote(red_s.at[k, r], red.at[k, r], rs.at[k, d], rr.at[k, r], here).wait_recv()

        loop(1, 16, one)
        return jnp.sum(red[k].astype(F32), axis=0)

    outs = (du_out, yp_out, dl_out)

    def spread(k, d):
        r, to = peer(d)
        return remote(outs[k].at[me], outs[k].at[me], gs.at[k, d], gr.at[k, me], to)

    def spread_end(k):
        def one(d):
            r, _ = peer(d)
            remote(outs[k].at[r], outs[k].at[r], gs.at[k, d], gr.at[k, r], here).wait_recv()

        loop(1, 16, one)

    def column(d):
        return remote(dcol.at[col], dcol.at[col], cs.at[d], cr.at[col], (g, row, (col + d) % 8))

    def upper_1():
        for c in range(8):
            chosen_s[c] = xs[parent[c]]
        loop(1, 16, lambda i: pick(i).start())
        ct[mine, lanes] = chosen_s[col, 0]

    def upper_2():
        wait_turned(xst.at[0], 0)
        x_out[...] = xst[0]
        reduce_start(0, flipped(masked[0], xst[0]))
        wait_turned(ct, 2)
        reduce_start(1, flipped(ct[...], masked[1]))
        cl[...] = jnp.dot(ct[...], lp[...], preferred_element_type=F32)

    def upper_3():
        du = (du_in[me] - reduce_end(0)).astype(BF16)
        du_out[me] = du
        dcol[col] = du
        loop(1, 8, lambda d: column(d).start())
        loop(1, 16, lambda d: spread(0, d).start())

    def upper_4():
        crossed = reduce_end(1)

        def one(d):
            c = (col + d) % 8
            remote(dcol.at[c], dcol.at[c], cs.at[d], cr.at[c], here).wait_recv()

        loop(1, 8, one)
        own = dcol[parent[col]]
        yp_out[me] = (-(crossed + jnp.dot(own, lp[...], preferred_element_type=F32))).astype(BF16)
        loop(1, 16, lambda d: spread(1, d).start())

    local_a.wait()
    swap_a.wait_recv()
    step_a(0)
    step_a(1)
    step_b(0)

    def body(n, carry):
        m = n // 2

        @pl.when((n < NS) & (n % 2 == 0))
        def _():
            pl.when(m + 2 < CH)(lambda: step_a(m + 2))
            pl.when(m + 1 < CH)(lambda: step_b(m + 1))
            step_w(m)

        pl.when(n < NS)(lambda: step_c(n))
        for lag, step in ((2, step_d), (4, step_e), (5, step_f)):
            k = n - lag
            pl.when((k >= 0) & (k < NS))(lambda step=step, k=k: step(k))
        for at, step in ((12, upper_1), (14, upper_2), (16, upper_3), (18, upper_4)):
            pl.when(n == at)(step)
        return carry

    lax.fori_loop(0, NS + 5, body, 0)

    wait_turned(xst.at[1], 1)
    y = (xst[1].astype(F32) - cl[...]).astype(BF16)
    y_out[...] = y
    reduce_start(2, flipped(masked[1], y))
    spread_end(1)
    back[...] = flipped(lp[...], yp_out[...].reshape(B, B)).reshape(16, B // 16, B)
    dl_out[me] = (dl_in[me] - reduce_end(2) - back[me]).astype(BF16)
    loop(1, 16, lambda d: spread(2, d).start())

    swap_a.wait_send()
    for pn in range(2):
        for dz, dg in order:
            if (dz, dg) != (0, 0):
                first(pn, dz, dg).wait_send()
        for way in far_first:
            if way != (0, 0, 0):
                second(pn, *way)[2].wait_send()

    def sent_chunk(m):
        for slot in range(6):
            gather(m, slot, z, 0, right).wait_send()

    loop(0, CH, sent_chunk)

    def sent_piece(n):
        for way in range(2):
            half_copy(n, way).wait_send()
            full_copy(n, way).wait_send()
        pair_copy(n).wait_send()

    loop(0, NS, sent_piece)

    def sent_turn(i):
        pick(i).wait_send()
        for pn in range(2):
            turn(pn, (col + i // 2) % 8, i % 2).wait_send()

    loop(1, 16, sent_turn)

    def sent_sum(d):
        for k in range(3):
            scatter(k, d).wait_send()
            spread(k, d).wait_send()

    loop(1, 16, sent_sum)
    loop(1, 8, lambda d: column(d).wait_send())
    spread_end(0)
    spread_end(2)


def step(a, lu, mask_u, du, ll, mask_l, parent, lp, dl):
    rows, depth = a.shape
    quarter, sl, deep = rows // 4, rows // 8, B // 16
    dma = pltpu.SemaphoreType.DMA
    vmem, smem = pl.BlockSpec(memory_space=pltpu.VMEM), pl.BlockSpec(memory_space=pltpu.SMEM)
    block = jax.ShapeDtypeStruct((rows, B), BF16)
    square = jax.ShapeDtypeStruct((16, deep, B), BF16)
    v = pltpu.VMEM
    x, y, d_u, y_p, d_l = pl.pallas_call(
        kernel,
        out_shape=(block, block, square, square, square),
        in_specs=[smem] * 3 + [vmem] * 2 + [pl.BlockSpec(memory_space=pl.ANY)] + [vmem] * 3,
        out_specs=(vmem,) * 5,
        scratch_shapes=[
            v((2, rows, B), BF16),
            v((2, rows, depth), BF16),
            v((2, 4, 2, quarter, H), BF16),
            v((CH, depth, B), BF16),
            v((NS, 4, 2, sl, B), BF16),
            v((NS, 2, sl, B), BF16),
            v((NS, 2, 2, sl, B), BF16),
            v((NS, sl, B), F32),
            v((NS, sl, B), BF16),
            v((16, 2, sl, H), BF16),
            v((8, 2, sl, H), BF16),
            v((2, rows, B), BF16),
            v((rows, B), BF16),
            v((rows, B), F32),
            v((3, 16, deep, B), BF16),
            v((3, 16, deep, B), BF16),
            v((8, deep, B), BF16),
            v((16, deep, B), F32),
            dma, dma, dma,
            dma((2, 8)), dma((2, 8)),
            dma((2, 16)), dma((2, 16)),
            dma((CH, 6)), dma((CH, 6)),
            dma((NS, 2)), dma((NS, 2)),
            dma((NS, 2)), dma((NS, 2)),
            dma((NS,)), dma((NS,)),
            dma((3, 16)), dma((3, 16)),
            dma((3, 16)), dma((3, 16)),
            dma((8,)), dma((8,)),
            dma((3, 16)), dma((3, 16)),
        ],
        compiler_params=pltpu.CompilerParams(has_side_effects=True, vmem_limit_bytes=60 * 2**20),
        name="levels",
    )(mask_u, mask_l, parent, lu, ll, a, lp, du.reshape(16, deep, B), dl.reshape(16, deep, B))
    return x, d_u.reshape(B, B), y, y_p.reshape(B, B), d_l.reshape(B, B)


def solution(mesh):
    rows, cols = P(("grp", "row"), "col"), P(None, "col")
    none = P(None, None)
    return jax.shard_map(
        step,
        mesh=mesh,
        in_specs=(rows, rows, none, cols, rows, none, P(None), cols, cols),
        out_specs=(rows, cols, rows, cols, cols),
        check_vma=False,
    )
```

time: 626 us -> 152 us (0.24)
  waiting for transfers between devices: 531 us -> 0 us
  Pallas kernels: 0 us -> 141 us
  matrix products: 24.4 us -> 0 us
  local copies, waits for them, and re-layouts: 31.5 us -> 8.23 us
  between operations: 16.9 us -> 0.64 us
  other arithmetic: 9.29 us -> 0 us
  starting transfers between devices: 7.42 us -> 0 us
    dot_general x3 -> x0, waiting for transfers between devices: 293 us -> none  [the longest x1 146 us: reference(): jnp.einsum('aub,auc->buc', upper_cube, x_cube, precision=precise)]
    pallas_call x0 -> x1, Pallas kernels: none -> 141 us  [step(): pl.pallas_call(kernel, out_shape=(block, block, square, square, square),...]
    unnamed x9 -> x0, waiting for transfers between devices: 129 us -> none
    reshape x2 -> x0, waiting for transfers between devices: 79.1 us -> none  [the longest x1 48.9 us: reference(): x_cube = x_upper.astype(jnp.float32).reshape(ANC, SN, B)]
    select_n x2 -> x0, waiting for transfers between devices: 30.6 us -> none  [masked_panel(): jnp.where(keeping, shaped, jnp.zeros((), factor.dtype))]
    dot_general x8 -> x0, matrix products: 24.4 us -> none  [the longest x1 7.01 us: reference(): jnp.dot(ancestor, lower_masked.astype(jnp.float32), precision=precise)]
    dot_general x2 -> x0, local copies, waits for them, and re-layouts: 12.7 us -> none  [the longest x1 6.36 us: reference(): jnp.dot(ancestor, upper_masked.astype(jnp.float32), precision=precise)]
    select_n x2 -> x0, starting transfers between devices: 6.95 us -> none  [masked_panel(): jnp.where(keeping, shaped, jnp.zeros((), factor.dtype))]
  transfers between devices with their start and end apart: 9 -> 0, of which waited for: 9 -> 0; matrix products, arithmetic and copies ran while one was open for 5% -> 0% of each run, Pallas kernels for 0% -> 0%
where the time goes in v2:
time: 152 us; the launch traced here: 150 us
  Pallas kernels  141 us (93%)
  local copies, waits for them, and re-layouts  8.23 us (5%)
    pallas_call x1, Pallas kernels, step(): pl.pallas_call(kernel, out_shape=(block, block, square, square, square),...  141 us
    unnamed x5, local copies, waits for them, and re-layouts  8.23 us

profile of v2, /device:TPU:1, one launch (start us, length us, event | category | flops | bytes accessed | tf_op | source)
XLA Modules:
  0.0 150.0 jit_solution(13766436591799693496)
XLA Ops:
  0.6 141.1 %levels.1 = (bf16[768,256]{1,0:T(8,128)(2,1)}, bf16[768,256]{1,0:T(8,128)(2,1)}, bf16[16,16,256]{2,1,0:T(8,128)(2,1)}, bf16[16,16,256]{2,1,0:T(8,128)(2,1)}, bf16[16,16,256]{2,1,0:T(8,128)(2,1)}) custom-call(s32[8,48]{1,0:T(8,128)} %mask_u.1, s32[8,48]{1,0:T(8,128)} %mask_l.1, s32[8]{0:T(128)} %parent.1, bf16[768,256]{1,0:T(8,128)(2,1)} %lu.1, ...), custom_call_target="tpu_custom_call" | custom-call | tf_op jit(solution)/shard_map/levels/pallas_call | solution.py:389
  141.8 1.8 %copy.19 = bf16[768,256]{1,0:T(8,128)(2,1)} copy(bf16[768,256]{1,0:T(8,128)(2,1)} %get-tuple-element.20) | data formatting | bytes 786432
  143.5 1.6 %copy.20 = bf16[256,256]{1,0:T(8,128)(2,1)} copy(bf16[256,256]{1,0:T(8,128)(2,1)} %bitcast.9) | data formatting | bytes 262144
  145.1 1.8 %copy.21 = bf16[768,256]{1,0:T(8,128)(2,1)} copy(bf16[768,256]{1,0:T(8,128)(2,1)} %get-tuple-element.22) | data formatting | bytes 786432
  146.9 1.6 %copy.22 = bf16[256,256]{1,0:T(8,128)(2,1)} copy(bf16[256,256]{1,0:T(8,128)(2,1)} %bitcast.8) | data formatting | bytes 262144
  148.4 1.6 %copy.23 = bf16[256,256]{1,0:T(8,128)(2,1)} copy(bf16[256,256]{1,0:T(8,128)(2,1)} %bitcast.7) | data formatting | bytes 262144

commit v3 on v2

v3 whole, which is shorter than its diff:
```python
import jax
import jax.numpy as jnp
from jax import lax
from jax.experimental import pallas as pl
from jax.experimental.pallas import tpu as pltpu
from jax.sharding import PartitionSpec as P

B = 256
H = 128
CH = 8
NS = 16
LAGS = (2, 4, 6)
UPPER = (13, 15)
AHEAD = (2, 1)
ORDER = 2
MESH = pl.DeviceIdType.MESH
F32 = jnp.float32
BF16 = jnp.bfloat16


def device(g, x, h, b, z):
    return (g, z * 2 + h, b * 4 + x)


def swapped(n):
    return n % 2 == 1


def remote(src, dst, send, recv, target):
    return pltpu.make_async_remote_copy(
        src_ref=src, dst_ref=dst, send_sem=send, recv_sem=recv, device_id=target, device_id_type=MESH
    )


def took(ref, sem, target):
    remote(ref, ref, sem, sem, target).wait_recv()


def left_here(ref, sem, target):
    remote(ref, ref, sem, sem, target).wait_send()


def aligned(start, size):
    return pl.ds(pl.multiple_of(start, size), size)


def loop(lo, hi, f):
    def body(i, carry):
        f(i)
        return carry

    lax.fori_loop(lo, hi, body, 0)


def flipped(p, q):
    return lax.dot_general(p, q, (((0,), (0,)), ((), ())), preferred_element_type=F32)


def kernel(
    mask_u_in, mask_l_in, parent_in, lu_in, ll_in, a_in, lp_in, du_arg, dl_arg,
    x_out, y_out, du_out, yp_out, dl_out,
    mask_u, mask_l, parent, lu, ll, lp, du_in, dl_in, masked, a, s1, panel, part, r1, r2, kept, yb, xs, chosen_s, xst, ct, cl, red_s, red, dcol, back,
    in_sem, as_sem, ar_sem, s1s, s1r, s2s, s2r, ags, agr, ps, p1r, p2r, p3r,
    ts, tr, rs, rr, cs, cr, gs, gr,
):
    g, row, col = lax.axis_index("grp"), lax.axis_index("row"), lax.axis_index("col")
    z, h, b, x = row // 2, row % 2, col // 4, col % 4
    me = g * 8 + row
    rows = a.shape[1]
    quarter, sl, half = rows // 4, rows // 8, rows // 2
    bl = min(B, rows)
    here = (g, row, col)

    arrivals_of = ((lu_in, lu), (ll_in, ll), (mask_u_in, mask_u), (mask_l_in, mask_l), (a_in, a.at[0]),
                   (parent_in, parent), (lp_in, lp), (du_arg, du_in), (dl_arg, dl_in))
    loads = [pltpu.make_async_copy(src, dst, in_sem.at[i]) for i, (src, dst) in enumerate(arrivals_of)]
    for load in loads:
        load.start()

    plane = [(0, dx, dy, 0) for dx in range(4) for dy in range(4)]
    line = [(dg, 0, dy, dz) for dg in range(2) for dy in (0, 2) for dz in range(4)]
    across = [(1, dx, db, 0) for dx in range(4) for db in (0, 5)]
    barrier = pltpu.get_barrier_semaphore()
    peers = []
    for dg, dx, dy, dz in plane + line + across:
        if dy == 5:
            key, ht, bt = (dg, dx, 5, dz), h, 1 - b
        else:
            y = (2 * h + b + dy) % 4
            key, ht, bt = (dg, dx, dy, dz), y // 2, y % 2
        if key != (0, 0, 0, 0) and key not in peers:
            peers.append(key)
            pl.semaphore_signal(
                barrier, inc=1, device_id=device((g + dg) % 2, (x + dx) % 4, ht, bt, (z + dz) % 4),
                device_id_type=MESH,
            )

    for load in loads[:4]:
        load.wait()
    for pn, (factor, mask) in enumerate(((lu, mask_u), (ll, mask_l))):
        for i in range(rows // bl):
            keep = mask[col, (me * rows + i * bl) // B] > 0
            values = factor[i * bl:(i + 1) * bl, :]
            masked[pn, i * bl:(i + 1) * bl, :] = jnp.where(keep, values, jnp.zeros_like(values))

    swap_a = remote(a.at[0], a.at[1], as_sem, ar_sem, (1 - g, row, col))
    pl.semaphore_wait(barrier, len(peers))

    def piece(pn, q, half_of):
        return masked.at[pn, aligned(q * quarter, quarter), aligned(half_of * H, H)]

    def first(pn, dz, dg):
        gt, zt = (g + dg) % 2, (z + dz) % 4
        return remote(
            piece(pn, zt, gt), s1.at[g, z, pn], s1s.at[pn], s1r.at[pn, g * 4 + z],
            device(gt, x, h, b, zt),
        )

    def first_in(pn, dz, dg):
        gf, zf = (g + dg) % 2, (z + dz) % 4
        return remote(piece(pn, z, g), s1.at[gf, zf, pn], s1s.at[pn], s1r.at[pn, gf * 4 + zf], here)

    order = [(dz, dg) for dz in (2, 1, 3, 0) for dg in (0, 1)]
    for pn in range(2):
        for dz, dg in order:
            if (dz, dg) != (0, 0):
                first(pn, dz, dg).start()
        s1[g, z, pn] = masked[pn, aligned(z * quarter, quarter), aligned(g * H, H)]

    def spot_from(pn, hf, cf, lane):
        return (pn * 4 + cf // 2, aligned(hf * rows + z * quarter, quarter), lane)

    def second(pn, dz, dg, dh):
        zf, gf, ht = (z + dz) % 4, (g + dg) % 2, (h + dh) % 2
        stays = (zf == x) & (gf == b) & (ht == h)
        return stays, zf, gf, remote(
            s1.at[gf, zf, pn], panel.at[spot_from(pn, h, col, aligned((col % 2) * H, H))],
            s2s.at[pn], s2r.at[pn * 4 + col // 2], device(g, zf, ht, gf, z),
        )

    arrivals = [(dz, dg) for dz in (0, 1, 3, 2) for dg in (0, 1)]
    def pass_on(pn):
        for dz, dg in arrivals:
            if (dz, dg) != (0, 0):
                first_in(pn, dz, dg).wait_recv()
            for dh in range(2):
                stays, zf, gf, copy = second(pn, dz, dg, dh)
                pl.when(jnp.logical_not(stays))(copy.start)

                @pl.when(stays)
                def _(zf=zf, gf=gf):
                    panel[spot_from(pn, h, col, aligned((col % 2) * H, H))] = s1[gf, zf, pn]

    pass_on(0)
    loads[4].wait()
    swap_a.start()

    right, left = device(g, x, h, b, (z + 1) % 4), device(g, x, h, b, (z + 3) % 4)

    def gather(m, kind, q, hf, to):
        spot = panel.at[m, aligned(hf * rows + q * quarter, quarter)]
        return remote(spot, spot, ags, agr.at[m, kind], to)

    def step_a(m):
        own = col // 2 == m % 4
        pl.when(own)(lambda: took(panel.at[m, pl.ds(0, 3 * quarter // 2)], s2r.at[m], here))
        pl.when(jnp.logical_not(own))(lambda: took(panel.at[m, pl.ds(0, 2 * quarter)], s2r.at[m], here))
        gather(m, 0, z, 0, right).start()
        gather(m, 1, z, 1, left).start()
        gather(m, 2, z, 1, right).start()
        gather(m, 2, z, 0, left).start()

    def step_b(m):
        gather(m, 0, (z + 3) % 4, 0, right).wait_recv()
        gather(m, 2, (z + 3) % 4, 0, right).start()
        gather(m, 1, (z + 1) % 4, 1, left).wait_recv()
        gather(m, 2, (z + 1) % 4, 1, left).start()

    def step_w(m):
        took(panel.at[m, pl.ds(0, rows)], agr.at[m, 2], here)

    xr, xl = device(g, (x + 1) % 4, h, b, z), device(g, (x + 3) % 4, h, b, z)
    yp = device(g, x, h, 1 - b, z)
    far_x = (x + 2) % 4
    low = sl // 2

    def near(way):
        return (x + 1 + 2 * way) % 4

    def x_copy(src, dst, arrived, way):
        return remote(src, dst, ps, arrived, xl if way else xr)

    def half_even(n, way):
        return x_copy(part.at[n, way, far_x], r1.at[n, way], p1r.at[n], way)

    def half_odd(n, way):
        return x_copy(part.at[n, b, far_x, pl.ds(way * low, low)], r1.at[n, 0, pl.ds(way * low, low)], p1r.at[n], way)

    def full_even(n, way):
        return x_copy(part.at[n, :, near(way)], r2.at[n, way], p2r.at[n], way)

    def full_odd(n, way):
        return x_copy(part.at[n, b, near(way)], r2.at[n, 0, way], p2r.at[n], way)

    def pair_even(n):
        return remote(r2.at[n, 0, 1 - b], yb.at[n, 0], ps, p3r.at[n], yp)

    def pair_odd(n):
        return remote(part.at[n, 1 - b], yb.at[n], ps, p3r.at[n], yp)

    def add(p, q):
        return (p.astype(F32) + q.astype(F32)).astype(BF16)

    def by_parity(n, even, odd):
        pl.when(jnp.logical_not(swapped(n)))(lambda: even(n))
        pl.when(swapped(n))(lambda: odd(n))

    def step_c(n):
        m, o = n // 2, n % 2
        for bt in range(2):
            product = jnp.dot(
                a[o, bt * half:(bt + 1) * half, :], panel[m], preferred_element_type=F32
            ).astype(BF16)
            for xt in range(4):
                part[n, bt, xt] = product[xt * sl:(xt + 1) * sl]

        def even(n):
            half_even(n, 0).start()
            half_even(n, 1).start()

        by_parity(n, even, lambda n: pair_odd(n).start())

    def step_d(n):
        def even(n):
            took(r1.at[n], p1r.at[n], here)
            for way in range(2):
                part[n, way, near(way)] = add(part[n, way, near(way)], r1[n, way])
            full_even(n, 0).start()
            full_even(n, 1).start()

        def odd(n):
            pair_odd(n).wait_recv()
            for xt in range(4):
                part[n, b, xt] = add(part[n, b, xt], yb[n, xt])
            half_odd(n, 0).start()
            half_odd(n, 1).start()

        by_parity(n, even, odd)

    def step_e(n):
        def even(n):
            took(r2.at[n], p2r.at[n], here)
            for bt in range(2):
                total = part[n, bt, x].astype(F32) + r2[n, 0, bt].astype(F32) + r2[n, 1, bt].astype(F32)
                r2[n, 0, bt] = total.astype(BF16)

                @pl.when(b == bt)
                def _():
                    kept[n] = total

            pair_even(n).start()

        def odd(n):
            took(r1.at[n, 0], p1r.at[n], here)
            for way in range(2):
                spot = (n, b, near(way), pl.ds(way * low, low))
                part[spot] = add(part[spot], r1[n, 0, way * low:(way + 1) * low])
            full_odd(n, 0).start()
            full_odd(n, 1).start()

        by_parity(n, even, odd)

    def finish(n):
        def even(n):
            pair_even(n).wait_recv()
            kept[n] = -(kept[n] + yb[n, 0].astype(F32))

        def odd(n):
            took(r2.at[n, 0], p2r.at[n], here)
            kept[n] = -(part[n, b, x].astype(F32) + r2[n, 0, 0].astype(F32) + r2[n, 0, 1].astype(F32))

        by_parity(n, even, odd)
        return kept[n].astype(BF16)

    mine, lanes = aligned(col * sl, sl), aligned(g * H, H)

    def turn(pn, c, o):
        return remote(
            xs.at[pn * 8 + c, o], xst.at[pn, mine, lanes], ts.at[pn], tr.at[pn],
            ((g + o) % 2, row, c),
        )

    def wait_turned(dst, k):
        took(dst.at[pl.ds(0, 15 * sl // 2)], tr.at[k], here)

    def step_f(n):
        m, o = n // 2, n % 2
        pn = n // 8
        result = finish(n)
        for e in range(2):
            xs[2 * m + e, o] = result[:, e * H:(e + 1) * H]
        for e in range(2):
            c = 2 * (m % 4) + e
            self_turn = (c == col) & (o == 0)
            pl.when(jnp.logical_not(self_turn))(turn(pn, c, o).start)

            @pl.when(self_turn)
            def _():
                xst[pn, mine, lanes] = result[:, e * H:(e + 1) * H]

    def pick(i):
        c, o = (col + i // 2) % 8, i % 2
        return remote(
            chosen_s.at[c, o], ct.at[mine, lanes], ts.at[2], tr.at[2], ((g + o) % 2, row, c)
        )

    def peer(d):
        r = (me + d) % 16
        return r, (r // 8, r % 8, col)

    def scatter(k, d):
        r, to = peer(d)
        return remote(red_s.at[k, r], red.at[k, me], rs.at[k], rr.at[k], to)

    def reduce_start(k, value):
        red_s[k] = value.reshape(16, B // 16, B).astype(BF16)
        loop(1, 16, lambda d: scatter(k, d).start())
        red[k, me] = red_s[k, me]

    def reduce_end(k):
        took(red.at[k, pl.ds(0, 15)], rr.at[k], here)
        return jnp.sum(red[k].astype(F32), axis=0)

    outs = (du_out, yp_out, dl_out)

    def spread(k, d):
        r, to = peer(d)
        return remote(outs[k].at[me], outs[k].at[me], gs.at[k], gr.at[k], to)

    def spread_end(k):
        took(outs[k].at[pl.ds(0, 15)], gr.at[k], here)

    def column(d):
        return remote(dcol.at[col], dcol.at[col], cs, cr, (g, row, (col + d) % 8))

    def upper_1():
        for c in range(8):
            chosen_s[c] = xs[parent[c]]
        loop(1, 16, lambda i: pick(i).start())
        ct[mine, lanes] = chosen_s[col, 0]

    def upper_2():
        wait_turned(xst.at[0], 0)
        x_out[...] = xst[0]
        reduce_start(0, flipped(masked[0], xst[0]))
        wait_turned(ct, 2)
        reduce_start(1, flipped(ct[...], masked[1]))
        cl[...] = jnp.dot(ct[...], lp[...], preferred_element_type=F32)

    def upper_3():
        du = (du_in[me] - reduce_end(0)).astype(BF16)
        du_out[me] = du
        dcol[col] = du
        loop(1, 8, lambda d: column(d).start())
        loop(1, 16, lambda d: spread(0, d).start())

    def upper_4():
        crossed = reduce_end(1)
        took(dcol.at[pl.ds(0, 7)], cr, here)
        own = dcol[parent[col]]
        yp_out[me] = (-(crossed + jnp.dot(own, lp[...], preferred_element_type=F32))).astype(BF16)
        loop(1, 16, lambda d: spread(1, d).start())

    for load in loads[5:]:
        load.wait()
    if ORDER == 0:
        pass_on(1)
    for m in range(AHEAD[0]):
        step_a(m)
    if ORDER == 1:
        pass_on(1)
    for m in range(AHEAD[1]):
        step_b(m)
    if ORDER == 2:
        pass_on(1)
    swap_a.wait_recv()

    def body(n, carry):
        m = n // 2

        @pl.when((n < NS) & (n % 2 == 0))
        def _():
            pl.when(m + AHEAD[0] < CH)(lambda: step_a(m + AHEAD[0]))
            pl.when(m + AHEAD[1] < CH)(lambda: step_b(m + AHEAD[1]))
            step_w(m)

        pl.when(n < NS)(lambda: step_c(n))
        for lag, step in zip(LAGS, (step_d, step_e, step_f)):
            k = n - lag
            pl.when((k >= 0) & (k < NS))(lambda step=step, k=k: step(k))
        for at, step in zip(UPPER, (upper_1, upper_2)):
            pl.when(n == at)(step)
        return carry

    lax.fori_loop(0, NS + LAGS[-1], body, 0)

    upper_3()
    wait_turned(xst.at[1], 1)
    y = (xst[1].astype(F32) - cl[...]).astype(BF16)
    y_out[...] = y
    reduce_start(2, flipped(masked[1], y))
    upper_4()
    lower = dl_in[me] - reduce_end(2)
    spread_end(1)
    back[...] = flipped(lp[...], yp_out[...].reshape(B, B)).reshape(16, B // 16, B)
    dl_out[me] = (lower - back[me]).astype(BF16)
    loop(1, 16, lambda d: spread(2, d).start())

    swap_a.wait_send()
    for pn in range(2):
        left_here(panel.at[0, pl.ds(0, 7 * quarter // 2)], s1s.at[pn], here)
        left_here(panel.at[0, pl.ds(0, 15 * quarter // 2)], s2s.at[pn], here)
    left_here(panel.at[pl.ds(0, 6)], ags, here)
    left_here(panel.at[pl.ds(0, 7)], ps, here)
    for k in range(3):
        left_here(ct.at[pl.ds(0, 15 * sl // 2)], ts.at[k], here)
        left_here(red_s.at[k, pl.ds(0, 15)], rs.at[k], here)
        left_here(outs[k].at[pl.ds(0, 15)], gs.at[k], here)
    left_here(dcol.at[pl.ds(0, 7)], cs, here)
    spread_end(0)
    spread_end(2)


def step(a, lu, mask_u, du, ll, mask_l, parent, lp, dl):
    rows, depth = a.shape
    quarter, sl, deep = rows // 4, rows // 8, B // 16
    dma = pltpu.SemaphoreType.DMA
    vmem = pl.BlockSpec(memory_space=pltpu.VMEM)
    block = jax.ShapeDtypeStruct((rows, B), BF16)
    square = jax.ShapeDtypeStruct((16, deep, B), BF16)
    v = pltpu.VMEM
    x, y, d_u, y_p, d_l = pl.pallas_call(
        kernel,
        out_shape=(block, block, square, square, square),
        in_specs=[pl.BlockSpec(memory_space=pltpu.HBM)] * 9,
        out_specs=(vmem,) * 5,
        scratch_shapes=[
            pltpu.SMEM(mask_u.shape, jnp.int32),
            pltpu.SMEM(mask_l.shape, jnp.int32),
            pltpu.SMEM(parent.shape, jnp.int32),
            v((rows, B), BF16),
            v((rows, B), BF16),
            v((B, B), BF16),
            v((16, deep, B), F32),
            v((16, deep, B), F32),
            v((2, rows, B), BF16),
            v((2, rows, depth), BF16),
            v((2, 4, 2, quarter, H), BF16),
            v((CH, depth, B), BF16),
            v((NS, 2, 4, sl, B), BF16),
            v((NS, 2, sl, B), BF16),
            v((NS, 2, 2, sl, B), BF16),
            v((NS, sl, B), F32),
            v((NS, 4, sl, B), BF16),
            v((16, 2, sl, H), BF16),
            v((8, 2, sl, H), BF16),
            v((2, rows, B), BF16),
            v((rows, B), BF16),
            v((rows, B), F32),
            v((3, 16, deep, B), BF16),
            v((3, 16, deep, B), BF16),
            v((8, deep, B), BF16),
            v((16, deep, B), F32),
            dma((9,)), dma, dma,
            dma((2,)), dma((2, 8)),
            dma((2,)), dma((CH,)),
            dma, dma((CH, 3)),
            dma, dma((NS,)), dma((NS,)), dma((NS,)),
            dma((3,)), dma((3,)),
            dma((3,)), dma((3,)),
            dma, dma,
            dma((3,)), dma((3,)),
        ],
        compiler_params=pltpu.CompilerParams(collective_id=0, has_side_effects=True, vmem_limit_bytes=60 * 2**20),
        name="levels",
    )(mask_u, mask_l, parent, lu, ll, a, lp, du.reshape(16, deep, B), dl.reshape(16, deep, B))
    return place((x, d_u.reshape(B, B), y, y_p.reshape(B, B), d_l.reshape(B, B)))


def place_kernel(*refs):
    n = (len(refs) - 2) // 3
    sources, outs, held, sems_in, sems_out = refs[:n], refs[n:2 * n], refs[2 * n:3 * n], refs[-2], refs[-1]
    ins = [pltpu.make_async_copy(sources[i], held[i], sems_in.at[i]) for i in range(n)]
    puts = [pltpu.make_async_copy(held[i], outs[i], sems_out.at[i]) for i in range(n)]
    for copy in ins:
        copy.start()
    for i in range(n):
        ins[i].wait()
        puts[i].start()
    for copy in puts:
        copy.wait()


def place(arrays):
    n = len(arrays)
    hbm = pl.BlockSpec(memory_space=pltpu.HBM)
    return pl.pallas_call(
        place_kernel,
        out_shape=tuple(jax.ShapeDtypeStruct(v.shape, v.dtype) for v in arrays),
        in_specs=[hbm] * n,
        out_specs=(hbm,) * n,
        scratch_shapes=[pltpu.VMEM(v.shape, v.dtype) for v in arrays]
        + [pltpu.SemaphoreType.DMA((n,)), pltpu.SemaphoreType.DMA((n,))],
        compiler_params=pltpu.CompilerParams(vmem_limit_bytes=60 * 2**20),
        name="place",
    )(*arrays)


def solution(mesh):
    rows, cols = P(("grp", "row"), "col"), P(None, "col")
    none = P(None, None)
    return jax.shard_map(
        step,
        mesh=mesh,
        in_specs=(rows, rows, none, cols, rows, none, P(None), cols, cols),
        out_specs=(rows, cols, rows, cols, cols),
        check_vma=False,
    )
```

time: 152 us -> 126 us (0.83); the launches traced: 150 us -> 126 us
  Pallas kernels: 141 us -> 125 us
  local copies, waits for them, and re-layouts: 8.23 us -> 0 us
    pallas_call x1, Pallas kernels: 141 us -> 123 us  [step(): pl.pallas_call(kernel, out_shape=(block, block, square, square, square),...]
    unnamed x5 -> x0, local copies, waits for them, and re-layouts: 8.23 us -> none
    pallas_call x0 -> x1, Pallas kernels: none -> 2.09 us  [place(): pl.pallas_call(place_kernel, out_shape=tuple((jax.ShapeDtypeStruct(v.shap...]
where the time goes in v3:
time: 126 us
  Pallas kernels  125 us (99%)
    pallas_call x1, Pallas kernels, step(): pl.pallas_call(kernel, out_shape=(block, block, square, square, square),...  123 us

profile of v3, /device:TPU:1, one launch (start us, length us, event | category | flops | bytes accessed | tf_op | source)
XLA Modules:
  0.0 126.1 jit_solution(5019345273434474538)
XLA Ops:
  0.6 123.4 %levels.1 = (bf16[768,256]{1,0:T(8,128)(2,1)}, bf16[768,256]{1,0:T(8,128)(2,1)}, bf16[16,16,256]{2,1,0:T(8,128)(2,1)}, bf16[16,16,256]{2,1,0:T(8,128)(2,1)}, bf16[16,16,256]{2,1,0:T(8,128)(2,1)}) custom-call(s32[8,48]{1,0:T(8,128)} %mask_u_in.1, s32[8,48]{1,0:T(8,128)} %mask_l_in.1, s32[8]{0:T(128)} %parent_in.1, bf16[768,256]{1,0:T(8,128)(2,1)} %lu_in.1, ...), custom_call_target="tpu_custom_call" | custom-call | tf_op jit(solution)/shard_map/levels/pallas_call | solution.py:442
  124.0 2.1 %place.1 = (bf16[768,256]{1,0:T(8,128)(2,1)}, bf16[256,256]{1,0:T(8,128)(2,1)}, bf16[768,256]{1,0:T(8,128)(2,1)}, bf16[256,256]{1,0:T(8,128)(2,1)}, bf16[256,256]{1,0:T(8,128)(2,1)}) custom-call(bf16[768,256]{1,0:T(8,128)(2,1)} %get-tuple-element.10.refs_0_, bf16[256,256]{1,0:T(8,128)(2,1)} %bitcast.7, bf16[768,256]{1,0:T(8,128)(2,1)} %get-tuple-element.12.refs_2_, ...), custom_call_target="tpu_custom_call" | custom-call | tf_op jit(solution)/shard_map/place/pallas_call | solution.py:507

commit v4 on v3

--- a/solution.py
+++ b/solution.py
@@ -10,9 +10,8 @@
 CH = 8
 NS = 16
 LAGS = (2, 4, 6)
-UPPER = (13, 15)
+UPPER = (13, 15, 19)
 AHEAD = (2, 1)
-ORDER = 2
 MESH = pl.DeviceIdType.MESH
 F32 = jnp.float32
 BF16 = jnp.bfloat16
@@ -59,8 +58,8 @@
 def kernel(
     mask_u_in, mask_l_in, parent_in, lu_in, ll_in, a_in, lp_in, du_arg, dl_arg,
     x_out, y_out, du_out, yp_out, dl_out,
-    mask_u, mask_l, parent, lu, ll, lp, du_in, dl_in, masked, a, s1, panel, part, r1, r2, kept, yb, xs, chosen_s, xst, ct, cl, red_s, red, dcol, back,
-    in_sem, as_sem, ar_sem, s1s, s1r, s2s, s2r, ags, agr, ps, p1r, p2r, p3r,
+    mask_u, mask_l, parent, lu, ll, lp, du_in, dl_in, masked, a, s1, panel, part, r1, r2, kept, yb, xs, chosen_s, xst, ct, cl, red_s, red, dcol, back, y_held, du_held, yp_held, dl_held,
+    in_sem, out_sem, as_sem, ar_sem, s1s, s1r, s2s, s2r, ags, agr, ps, p1r, p2r, p3r,
     ts, tr, rs, rr, cs, cr, gs, gr,
 ):
     g, row, col = lax.axis_index("grp"), lax.axis_index("row"), lax.axis_index("col")
@@ -121,11 +120,14 @@
         return remote(piece(pn, z, g), s1.at[gf, zf, pn], s1s.at[pn], s1r.at[pn, gf * 4 + zf], here)
 
     order = [(dz, dg) for dz in (2, 1, 3, 0) for dg in (0, 1)]
-    for pn in range(2):
+    def hand_out(pn):
         for dz, dg in order:
             if (dz, dg) != (0, 0):
                 first(pn, dz, dg).start()
         s1[g, z, pn] = masked[pn, aligned(z * quarter, quarter), aligned(g * H, H)]
+
+    hand_out(0)
+    hand_out(1)
 
     def spot_from(pn, hf, cf, lane):
         return (pn * 4 + cf // 2, aligned(hf * rows + z * quarter, quarter), lane)
@@ -331,7 +333,13 @@
         took(red.at[k, pl.ds(0, 15)], rr.at[k], here)
         return jnp.sum(red[k].astype(F32), axis=0)
 
-    outs = (du_out, yp_out, dl_out)
+    outs = (du_held, yp_held, dl_held)
+    x_put, y_put, du_put, yp_put, dl_put = [
+        pltpu.make_async_copy(src, dst, out_sem.at[i])
+        for i, (src, dst) in enumerate(
+            ((xst.at[0], x_out), (y_held, y_out), (du_held, du_out), (yp_held, yp_out), (dl_held, dl_out))
+        )
+    ]
 
     def spread(k, d):
         r, to = peer(d)
@@ -351,7 +359,7 @@
 
     def upper_2():
         wait_turned(xst.at[0], 0)
-        x_out[...] = xst[0]
+        x_put.start()
         reduce_start(0, flipped(masked[0], xst[0]))
         wait_turned(ct, 2)
         reduce_start(1, flipped(ct[...], masked[1]))
@@ -359,7 +367,7 @@
 
     def upper_3():
         du = (du_in[me] - reduce_end(0)).astype(BF16)
-        du_out[me] = du
+        du_held[me] = du
         dcol[col] = du
         loop(1, 8, lambda d: column(d).start())
         loop(1, 16, lambda d: spread(0, d).start())
@@ -368,53 +376,54 @@
         crossed = reduce_end(1)
         took(dcol.at[pl.ds(0, 7)], cr, here)
         own = dcol[parent[col]]
-        yp_out[me] = (-(crossed + jnp.dot(own, lp[...], preferred_element_type=F32))).astype(BF16)
+        held = (-(crossed + jnp.dot(own, lp[...], preferred_element_type=F32))).astype(BF16)
+        yp_held[me] = held
         loop(1, 16, lambda d: spread(1, d).start())
+        back[...] = flipped(lp[aligned(me * (B // 16), B // 16), :], held)
 
     for load in loads[5:]:
         load.wait()
-    if ORDER == 0:
-        pass_on(1)
-    for m in range(AHEAD[0]):
-        step_a(m)
-    if ORDER == 1:
-        pass_on(1)
-    for m in range(AHEAD[1]):
-        step_b(m)
-    if ORDER == 2:
-        pass_on(1)
+    step_a(0)
+    step_a(1)
+    step_b(0)
+    pass_on(1)
     swap_a.wait_recv()
 
     def body(n, carry):
         m = n // 2
-
-        @pl.when((n < NS) & (n % 2 == 0))
+        starts = (n < NS) & (n % 2 == 0)
+
+        def late():
+            for lag, step in zip(LAGS, (step_d, step_e, step_f)):
+                k = n - lag
+                pl.when((k >= 0) & (k < NS))(lambda step=step, k=k: step(k))
+            for at, step in zip(UPPER, (upper_1, upper_2, upper_3)):
+                pl.when(n == at)(step)
+
+        @pl.when(starts)
         def _():
             pl.when(m + AHEAD[0] < CH)(lambda: step_a(m + AHEAD[0]))
             pl.when(m + AHEAD[1] < CH)(lambda: step_b(m + AHEAD[1]))
-            step_w(m)
-
+
+        pl.when(starts)(lambda: step_w(m))
         pl.when(n < NS)(lambda: step_c(n))
-        for lag, step in zip(LAGS, (step_d, step_e, step_f)):
-            k = n - lag
-            pl.when((k >= 0) & (k < NS))(lambda step=step, k=k: step(k))
-        for at, step in zip(UPPER, (upper_1, upper_2)):
-            pl.when(n == at)(step)
+        late()
         return carry
 
     lax.fori_loop(0, NS + LAGS[-1], body, 0)
 
-    upper_3()
+    upper_4()
     wait_turned(xst.at[1], 1)
     y = (xst[1].astype(F32) - cl[...]).astype(BF16)
-    y_out[...] = y
-    reduce_start(2, flipped(masked[1], y))
-    upper_4()
-    lower = dl_in[me] - reduce_end(2)
+    y_held[...] = y
+    y_put.start()
+    reduce_start(2, flipped(masked[1], y) + back[...])
+    dl_held[me] = (dl_in[me] - reduce_end(2)).astype(BF16)
+    loop(1, 16, lambda d: spread(2, d).start())
+    spread_end(0)
+    du_put.start()
     spread_end(1)
-    back[...] = flipped(lp[...], yp_out[...].reshape(B, B)).reshape(16, B // 16, B)
-    dl_out[me] = (lower - back[me]).astype(BF16)
-    loop(1, 16, lambda d: spread(2, d).start())
+    yp_put.start()
 
     swap_a.wait_send()
     for pn in range(2):
@@ -427,15 +436,16 @@
         left_here(red_s.at[k, pl.ds(0, 15)], rs.at[k], here)
         left_here(outs[k].at[pl.ds(0, 15)], gs.at[k], here)
     left_here(dcol.at[pl.ds(0, 7)], cs, here)
-    spread_end(0)
     spread_end(2)
+    dl_put.start()
+    for put in (x_put, y_put, du_put, yp_put, dl_put):
+        put.wait()
 
 
 def step(a, lu, mask_u, du, ll, mask_l, parent, lp, dl):
     rows, depth = a.shape
     quarter, sl, deep = rows // 4, rows // 8, B // 16
     dma = pltpu.SemaphoreType.DMA
-    vmem = pl.BlockSpec(memory_space=pltpu.VMEM)
     block = jax.ShapeDtypeStruct((rows, B), BF16)
     square = jax.ShapeDtypeStruct((16, deep, B), BF16)
     v = pltpu.VMEM
@@ -443,7 +453,7 @@
         kernel,
         out_shape=(block, block, square, square, square),
         in_specs=[pl.BlockSpec(memory_space=pltpu.HBM)] * 9,
-        out_specs=(vmem,) * 5,
+        out_specs=(pl.BlockSpec(memory_space=pltpu.HBM),) * 5,
         scratch_shapes=[
             pltpu.SMEM(mask_u.shape, jnp.int32),
             pltpu.SMEM(mask_l.shape, jnp.int32),
@@ -470,8 +480,12 @@
             v((3, 16, deep, B), BF16),
             v((3, 16, deep, B), BF16),
             v((8, deep, B), BF16),
-            v((16, deep, B), F32),
-            dma((9,)), dma, dma,
+            v((B, B), F32),
+            v((rows, B), BF16),
+            v((16, deep, B), BF16),
+            v((16, deep, B), BF16),
+            v((16, deep, B), BF16),
+            dma((9,)), dma((5,)), dma, dma,
             dma((2,)), dma((2, 8)),
             dma((2,)), dma((CH,)),
             dma, dma((CH, 3)),

time: 126 us -> 124 us (0.984)
    pallas_call x1, Pallas kernels: 123 us -> 121 us  [step(): pl.pallas_call(kernel, out_shape=(block, block, square, square, square),...]
where the time goes in v4:
time: 124 us
  Pallas kernels  124 us (100%)
    pallas_call x1, Pallas kernels, step(): pl.pallas_call(kernel, out_shape=(block, block, square, square, square),...  121 us

profile of v4, /device:TPU:1, one launch (start us, length us, event | category | flops | bytes accessed | tf_op | source)
XLA Modules:
  0.0 124.2 jit_solution(18407990944247053680)
XLA Ops:
  0.6 121.4 %levels.1 = (bf16[768,256]{1,0:T(8,128)(2,1)}, bf16[768,256]{1,0:T(8,128)(2,1)}, bf16[16,16,256]{2,1,0:T(8,128)(2,1)}, bf16[16,16,256]{2,1,0:T(8,128)(2,1)}, bf16[16,16,256]{2,1,0:T(8,128)(2,1)}) custom-call(s32[8,48]{1,0:T(8,128)} %mask_u_in.1, s32[8,48]{1,0:T(8,128)} %mask_l_in.1, s32[8]{0:T(128)} %parent_in.1, bf16[768,256]{1,0:T(8,128)(2,1)} %lu_in.1, ...), custom_call_target="tpu_custom_call" | custom-call | tf_op jit(solution)/shard_map/levels/pallas_call | solution.py:452
  122.1 2.1 %place.1 = (bf16[768,256]{1,0:T(8,128)(2,1)}, bf16[256,256]{1,0:T(8,128)(2,1)}, bf16[768,256]{1,0:T(8,128)(2,1)}, bf16[256,256]{1,0:T(8,128)(2,1)}, bf16[256,256]{1,0:T(8,128)(2,1)}) custom-call(bf16[768,256]{1,0:T(8,128)(2,1)} %get-tuple-element.10.refs_0_, bf16[256,256]{1,0:T(8,128)(2,1)} %bitcast.7, bf16[768,256]{1,0:T(8,128)(2,1)} %get-tuple-element.12.refs_2_, ...), custom_call_target="tpu_custom_call" | custom-call | tf_op jit(solution)/shard_map/place/pallas_call | solution.py:521

commit v5 on v4

--- a/solution.py
+++ b/solution.py
@@ -10,7 +10,7 @@
 CH = 8
 NS = 16
 LAGS = (2, 4, 6)
-UPPER = (13, 15, 19)
+UPPER = (13, 15, 18)
 AHEAD = (2, 1)
 MESH = pl.DeviceIdType.MESH
 F32 = jnp.float32

time: 124 us -> 124 us (level)
  no operation moved by 1% of the time
where the time goes in v5:
time: 124 us; the launch traced here: 123 us
  Pallas kernels  123 us (99%)
    pallas_call x1, Pallas kernels, step(): pl.pallas_call(kernel, out_shape=(block, block, square, square, square),...  121 us

profile of v5, /device:TPU:1, one launch (start us, length us, event | category | flops | bytes accessed | tf_op | source)
XLA Modules:
  0.0 123.3 jit_solution(1383160391176921833)
XLA Ops:
  0.6 120.6 %levels.1 = (bf16[768,256]{1,0:T(8,128)(2,1)}, bf16[768,256]{1,0:T(8,128)(2,1)}, bf16[16,16,256]{2,1,0:T(8,128)(2,1)}, bf16[16,16,256]{2,1,0:T(8,128)(2,1)}, bf16[16,16,256]{2,1,0:T(8,128)(2,1)}) custom-call(s32[8,48]{1,0:T(8,128)} %mask_u_in.1, s32[8,48]{1,0:T(8,128)} %mask_l_in.1, s32[8]{0:T(128)} %parent_in.1, bf16[768,256]{1,0:T(8,128)(2,1)} %lu_in.1, ...), custom_call_target="tpu_custom_call" | custom-call | tf_op jit(solution)/shard_map/levels/pallas_call | solution.py:452
  121.2 2.1 %place.1 = (bf16[768,256]{1,0:T(8,128)(2,1)}, bf16[256,256]{1,0:T(8,128)(2,1)}, bf16[768,256]{1,0:T(8,128)(2,1)}, bf16[256,256]{1,0:T(8,128)(2,1)}, bf16[256,256]{1,0:T(8,128)(2,1)}) custom-call(bf16[768,256]{1,0:T(8,128)(2,1)} %get-tuple-element.10.refs_0_, bf16[256,256]{1,0:T(8,128)(2,1)} %bitcast.7, bf16[768,256]{1,0:T(8,128)(2,1)} %get-tuple-element.12.refs_2_, ...), custom_call_target="tpu_custom_call" | custom-call | tf_op jit(solution)/shard_map/place/pallas_call | solution.py:521

commit v6 on v5

--- a/solution.py
+++ b/solution.py
@@ -317,7 +317,7 @@
         )
 
     def peer(d):
-        r = (me + d) % 16
+        r = (me + 5 * d) % 16
         return r, (r // 8, r % 8, col)
 
     def scatter(k, d):

time: 124 us -> 124 us (level)
  no operation moved by 1% of the time
where the time goes in v6:
time: 124 us
  Pallas kernels  123 us (99%)
    pallas_call x1, Pallas kernels, step(): pl.pallas_call(kernel, out_shape=(block, block, square, square, square),...  121 us

profile of v6, /device:TPU:1, one launch (start us, length us, event | category | flops | bytes accessed | tf_op | source)
XLA Modules:
  0.0 123.7 jit_solution(18345223742693324149)
XLA Ops:
  0.6 120.9 %levels.1 = (bf16[768,256]{1,0:T(8,128)(2,1)}, bf16[768,256]{1,0:T(8,128)(2,1)}, bf16[16,16,256]{2,1,0:T(8,128)(2,1)}, bf16[16,16,256]{2,1,0:T(8,128)(2,1)}, bf16[16,16,256]{2,1,0:T(8,128)(2,1)}) custom-call(s32[8,48]{1,0:T(8,128)} %mask_u_in.1, s32[8,48]{1,0:T(8,128)} %mask_l_in.1, s32[8]{0:T(128)} %parent_in.1, bf16[768,256]{1,0:T(8,128)(2,1)} %lu_in.1, ...), custom_call_target="tpu_custom_call" | custom-call | tf_op jit(solution)/shard_map/levels/pallas_call | solution.py:452
  121.6 2.1 %place.1 = (bf16[768,256]{1,0:T(8,128)(2,1)}, bf16[256,256]{1,0:T(8,128)(2,1)}, bf16[768,256]{1,0:T(8,128)(2,1)}, bf16[256,256]{1,0:T(8,128)(2,1)}, bf16[256,256]{1,0:T(8,128)(2,1)}) custom-call(bf16[768,256]{1,0:T(8,128)(2,1)} %get-tuple-element.10.refs_0_, bf16[256,256]{1,0:T(8,128)(2,1)} %bitcast.7, bf16[768,256]{1,0:T(8,128)(2,1)} %get-tuple-element.12.refs_2_, ...), custom_call_target="tpu_custom_call" | custom-call | tf_op jit(solution)/shard_map/place/pallas_call | solution.py:521
